TPU v7x, 128 devices: a whole 4x4x4 slice. The times are simulated.
128 devices in a mesh: lat: 2 (over core), lev: 64 (over z, y, x).
Axes of the slice: x: 4, y: 4, z: 4, core: 2. Of those that a mesh axis runs over, the one named last changes fastest.
Arguments:
- potential_temp: float32 [16, 128, 5760], P('lat', 'lev'), may hold values from 0.5 to 2
- layer_thickness: float32 [16, 128, 5760], P('lat', 'lev'), as said below
- zonal_wind: float32 [16, 128, 5760], P('lat', 'lev'), may hold values from -6 to 6
- meridional_wind: float32 [16, 128, 5760], P('lat', 'lev'), may hold values from -6 to 6
- surface_height: float32 [16, 5760], P('lat'), may hold values from 0 to 2
- target_eta: float32 [129], replicated, may hold values from 0 to 1, as said below
- intersection: int32 [3, 2, 128, 2, 64], P(None, None, None, 'lat', 'lev'), may hold values from 0 to 127, as said below
Outputs:
- remapped_temp: float32 [16, 128, 5760], P('lat', 'lev')
- remapped_thickness: float32 [16, 128, 5760], P('lat', 'lev')
- remapped_zonal: float32 [16, 128, 5760], P('lat', 'lev')
- remapped_meridional: float32 [16, 128, 5760], P('lat', 'lev')
- geopotential: float32 [16, 128, 5760], P('lat', 'lev')
Inputs may be any that keep to these rules, and one draw needn't show every extreme that they name: `layer_thickness`: every entry is positive. `target_eta`: strictly increasing, 0 at index 0 and 1 at index 128. intersection[kind, 0, k, b, c] is the first and intersection[kind, 1, k, b, c] the number of consecutive source layers that contain every source layer intersecting target layer k, in every column of block (b, c): latitude rows b * 8 to (b + 1) * 8 - 1 and longitudes c * 90 to (c + 1) * 90 - 1, for the edge set of that kind. Counts run from 1 to 3, and 3 is reached in every block; first plus count never exceeds 128.
All inputs are finite; a program needn't handle non-finite values.
Results may differ from a plain program's by a relative error of at most 0.0003.
Values sent between devices are 32-bit elements; how exact they have to be, the bound alone decides.
A program may use at most 128 MiB of HBM per device.

v0:
```python
import jax
import jax.numpy as jnp
from jax import lax
from jax.sharding import Mesh
from jax.sharding import PartitionSpec as P

WINDOW = 3
LEV = ("lev_0", "lev_1", "lev_2")


pressure_top = 0.2
kappa_power = 0.2857


def nothing_yet(shard, identity):
    return jnp.zeros_like(shard) + jnp.asarray(identity, shard.dtype)


def carried_in(shard, axes, combine, identity, reverse):
    before = start = nothing_yet(shard, identity)
    running = shard
    for axis in reversed(axes):
        peers, mine = (lax.axis_size(axis), lax.axis_index(axis))
        pieces = lax.all_gather(running, axis)
        inside, running = (start, start)
        for k in reversed(range(peers)) if reverse else range(peers):
            passed = k > mine if reverse else k < mine
            running = combine(running, pieces[k])
            inside = jnp.where(passed, running, inside)
        before = combine(inside, before)
    return before


def side_by_side(arrays, axis, split_dim, concat_dim, along):
    widths = [a.shape[along] for a in arrays]
    both = jnp.concatenate(arrays, axis=along)
    whole = lax.all_to_all(both, axis, split_axis=split_dim, concat_axis=concat_dim, tiled=True)
    return tuple(jnp.split(whole, [sum(widths[:k]) for k in range(1, len(widths))], axis=along))


def shifted(shard, axis, by):
    peers = lax.axis_size(axis)
    pairs = [(i, i + by) for i in range(peers) if 0 <= i + by < peers]
    return lax.ppermute(shard, axis, pairs)


def shifted_2(block, axis, distance):
    devices = range(lax.axis_size(axis))
    route = [((i - distance) % len(devices), i) for i in devices]
    return lax.ppermute(block, axis, route)


def piece_integral(left_edge, slope_term, curvature, lower_frac, upper_frac):
    span_one = upper_frac - lower_frac
    span_two = upper_frac * upper_frac - lower_frac * lower_frac
    span_three = upper_frac * upper_frac * upper_frac - lower_frac * lower_frac * lower_frac
    return (
        left_edge * span_one
        + 0.5 * slope_term * span_two
        + curvature * (0.5 * span_two - span_three / 3.0)
    )


def remap_block(values, edge_press, target_eta, starts, counts):
    layer_depth = edge_press[:, 1:] - edge_press[:, :-1]
    interface = (layer_depth[:, 1:] * values[:, :-1] + layer_depth[:, :-1] * values[:, 1:]) / (
        layer_depth[:, :-1] + layer_depth[:, 1:]
    )
    left_edge = jnp.concatenate([values[:, :1], interface], 1)
    right_edge = jnp.concatenate([interface, values[:, -1:]], 1)
    slope_term = right_edge - left_edge
    curvature = 6.0 * (values - 0.5 * (left_edge + right_edge))
    surface_span = edge_press[:, -1:] - pressure_top
    target = pressure_top + target_eta[None, :, None] * surface_span
    target_depth = (target_eta[1:] - target_eta[:-1])[None, :, None] * surface_span
    levels = values.shape[1]
    layer_ids = jnp.arange(levels, dtype=jnp.int32)
    stacked = jnp.stack([edge_press[:, :-1], layer_depth, left_edge, slope_term, curvature], 0)
    accumulated = jnp.zeros_like(values)
    for offset in range(WINDOW):
        source_layer = jnp.clip(starts + offset, 0, levels - 1)
        picker = (source_layer[:, None] == layer_ids[None, :]).astype(jnp.float32)
        picked = jnp.einsum("ks,frsc->frkc", picker, stacked, precision=lax.Precision.HIGHEST)
        source_top = picked[0]
        source_depth = picked[1]
        lower_frac = jnp.clip((target[:, :-1] - source_top) / source_depth, 0.0, 1.0)
        upper_frac = jnp.clip((target[:, 1:] - source_top) / source_depth, 0.0, 1.0)
        integral = piece_integral(picked[2], picked[3], picked[4], lower_frac, upper_frac)
        accumulated = accumulated + jnp.where(
            (offset < counts)[None, :, None], source_depth * integral, 0.0
        )
    return (accumulated / target_depth, target_depth)


def on_device(
    potential_temp,
    layer_thickness,
    zonal_wind,
    meridional_wind,
    surface_height,
    target_eta,
    intersection,
):
    column_part = jnp.sum(layer_thickness, axis=1)
    zero_part = jnp.zeros_like(column_part)
    pressure_above = carried_in(column_part, LEV, jnp.add, zero_part, False)
    inner_sums = jnp.cumsum(layer_thickness, axis=1)
    local_edges = (
        pressure_top
        + pressure_above[:, None, :]
        + jnp.concatenate([zero_part[:, None], inner_sums], 1)
    )
    edge_power = jnp.power(local_edges, kappa_power)
    layer_work = potential_temp * (edge_power[:, 1:] - edge_power[:, :-1])
    work_part = jnp.sum(layer_work, axis=1)
    work_below = carried_in(work_part, LEV, jnp.add, zero_part, True)
    geopotential = (
        surface_height[:, None, :]
        + work_below[:, None, :]
        + lax.cumsum(layer_work, axis=1, reverse=True)
    )
    exchanged = side_by_side(
        (potential_temp, layer_thickness, zonal_wind, meridional_wind), LEV, 2, 1, 0
    )
    column_temp, column_depth, column_zonal, column_merid = exchanged
    levels = column_depth.shape[1]
    lower_tri = (jnp.arange(levels + 1)[:, None] > jnp.arange(levels)[None, :]).astype(jnp.float32)
    edge_press = pressure_top + jnp.einsum(
        "ek,rkc->rec", lower_tri, column_depth, precision=lax.Precision.HIGHEST
    )
    south_row = shifted(edge_press[-1, 1:, :], "lat", 1)
    south_full = jnp.concatenate(
        [jnp.full((1, south_row.shape[1]), pressure_top, jnp.float32), south_row], 0
    )
    previous = jnp.concatenate([south_full[None], edge_press[:-1]], 0)
    row_ids = jnp.arange(edge_press.shape[0])
    at_start = jnp.logical_and(lax.axis_index("lat") == 0, row_ids == 0)
    previous = jnp.where(at_start[:, None, None], edge_press, previous)
    zonal_edges = 0.5 * (previous + edge_press)
    west_cols = shifted_2(edge_press[:, 1:, -1], LEV, 1)
    west_full = jnp.concatenate(
        [jnp.full((west_cols.shape[0], 1), pressure_top, jnp.float32), west_cols], 1
    )
    west_block = jnp.concatenate([west_full[:, :, None], edge_press[:, :, :-1]], 2)
    merid_edges = 0.5 * (west_block + edge_press)
    starts = intersection[:, 0, :, 0, 0]
    counts = intersection[:, 1, :, 0, 0]
    new_temp, new_depth = remap_block(column_temp, edge_press, target_eta, starts[0], counts[0])
    new_zonal, unused_one = remap_block(column_zonal, zonal_edges, target_eta, starts[1], counts[1])
    new_merid, unused_two = remap_block(column_merid, merid_edges, target_eta, starts[2], counts[2])
    returned = side_by_side((new_temp, new_zonal, new_merid, new_depth), LEV, 1, 2, 0)
    out_temp, out_zonal, out_merid, out_depth = returned
    return (out_temp, out_depth, out_zonal, out_merid, geopotential)


def solution(mesh):
    torus = Mesh(
        mesh.devices.reshape(mesh.shape["lat"], 4, 4, 4), ("lat", "lev_0", "lev_1", "lev_2")
    )
    in_specs = (
        P("lat", LEV, None),
        P("lat", LEV, None),
        P("lat", LEV, None),
        P("lat", LEV, None),
        P("lat", None),
        P(),
        P(None, None, None, "lat", LEV),
    )
    out_specs = (
        P("lat", LEV, None),
        P("lat", LEV, None),
        P("lat", LEV, None),
        P("lat", LEV, None),
        P("lat", LEV, None),
    )
    return jax.shard_map(
        on_device, mesh=torus, in_specs=in_specs, out_specs=out_specs, check_vma=False
    )
```

profile of v0, /device:TPU:0, one launch (start us, length us, event | category | flops | bytes accessed | tf_op | source)
XLA Modules:
  0.0 288.8 jit_solution(11124375768316120548)
XLA Ops:
  0.6 7.0 %copy.275 = f32[8,2,5760]{0,1,2:T(2,128)} copy(f32[8,2,5760]{2,1,0:T(2,128)} %param.7) | data formatting | bytes 737280 | tf_op args[0]
  7.6 5.5 %copy.276 = f32[8,2,5760]{0,1,2:T(2,128)} copy(f32[8,2,5760]{2,1,0:T(2,128)S(1)} %copy-done.9) | data formatting | bytes 737280 | tf_op args[1]
  13.1 5.5 %copy.277 = f32[8,2,5760]{0,1,2:T(2,128)} copy(f32[8,2,5760]{2,1,0:T(2,128)S(1)} %copy-done.14) | data formatting | bytes 737280 | tf_op args[2]
  18.6 5.5 %copy.278 = f32[8,2,5760]{0,1,2:T(2,128)} copy(f32[8,2,5760]{2,1,0:T(2,128)S(1)} %copy-done.15) | data formatting | bytes 737280 | tf_op args[3]
  24.1 21.8 %fusion.170 = f32[5760,2,32]{2,1,0:T(2,128)} fusion(f32[8,2,5760]{0,1,2:T(2,128)} %copy.278, f32[8,2,5760]{0,1,2:T(2,128)} %copy.277, f32[8,2,5760]{0,1,2:T(2,128)} %copy.276, f32[8,2,5760]{0,1,2:T(2,128)} %copy.275), kind=kLoop, calls=%fused_computation.344 | loop fusion | flops 1105920 | bytes 2949120
  45.9 8.3 %reshape.789 = f32[64,1,5760]{2,1,0:T(1,128)} reshape(f32[5760,2,32]{2,1,0:T(2,128)} %fusion.170) | data formatting | bytes 2949120
  54.1 11.7 %all-to-all-start = ((f32[64,1,5760]{2,1,0:T(1,128)}), f32[64,1,5760]{2,1,0:T(1,128)S(1)}, u32[]{:S(2)}, u32[]{:S(2)}) async-start(f32[64,1,5760]{2,1,0:T(1,128)} %reshape.789), calls=%async_computation | async-start | bytes 2949120 | tf_op jit(solution)/shard_map/all_to_all | solution.py:37
  67.5 1.6 reduce_window_sum.21
  69.8 24.3 %all-gather = f32[32,5760]{1,0:T(8,128)S(1)} all-gather(f32[8,5760]{1,0:T(8,128)S(1)} %reduce_sum.18), channel_id=2, replica_groups=mesh['lat'=2,'lev_0'=4,'lev_1'=4,'lev_2'=4] {'lev_2'}, dimensions={0}, use_global_device_ids=true | all-gather | bytes 921600 | tf_op jit(solution)/shard_map/all_gather | solution.py:24
  94.1 13.9 %all_gather.30 = f32[4,8,5760]{2,1,0:T(8,128)S(1)} all-gather(f32[1,8,5760]{2,1,0:T(8,128)S(1)} %fusion.128), channel_id=1, replica_groups=mesh['lat'=2,'lev_0'=4,'lev_1'=4,'lev_2'=4] {'lev_1'}, dimensions={0}, use_global_device_ids=true | all-gather | bytes 921600 | tf_op jit(solution)/shard_map/all_gather | solution.py:24
  108.0 13.8 %all_gather.31 = f32[4,8,5760]{2,1,0:T(8,128)S(1)} all-gather(f32[1,8,5760]{2,1,0:T(8,128)S(1)} %slice_add_fusion.12), channel_id=1, replica_groups=mesh['lat'=2,'lev_0'=4,'lev_1'=4,'lev_2'=4] {'lev_0'}, dimensions={0}, use_global_device_ids=true | all-gather | bytes 921600 | tf_op jit(solution)/shard_map/all_gather | solution.py:24
  123.5 13.2 %all-gather.1 = f32[32,5760]{1,0:T(8,128)S(1)} all-gather(f32[8,5760]{1,0:T(8,128)S(1)} %get-tuple-element.5), channel_id=3, replica_groups=mesh['lat'=2,'lev_0'=4,'lev_1'=4,'lev_2'=4] {'lev_2'}, dimensions={0}, use_global_device_ids=true | all-gather | bytes 921600 | tf_op jit(solution)/shard_map/all_gather | solution.py:24
  137.6 13.2 %all_gather.34 = f32[4,8,5760]{2,1,0:T(8,128)S(1)} all-gather(f32[1,8,5760]{2,1,0:T(8,128)S(1)} %fusion.123), channel_id=1, replica_groups=mesh['lat'=2,'lev_0'=4,'lev_1'=4,'lev_2'=4] {'lev_1'}, dimensions={0}, use_global_device_ids=true | all-gather | bytes 921600 | tf_op jit(solution)/shard_map/all_gather | solution.py:24
  151.8 24.2 %all_gather.35 = f32[4,8,5760]{2,1,0:T(8,128)} all-gather(f32[1,8,5760]{2,1,0:T(8,128)S(1)} %slice_add_fusion.3), channel_id=1, replica_groups=mesh['lat'=2,'lev_0'=4,'lev_1'=4,'lev_2'=4] {'lev_0'}, dimensions={0}, use_global_device_ids=true | all-gather | bytes 921600 | tf_op jit(solution)/shard_map/all_gather | solution.py:24
  176.5 4.1 %reduce.2 = f32[64,5760]{1,0:T(8,128)S(1)} reduce(f32[64,1,5760]{2,1,0:T(1,128)S(1)} %all-to-all-done, f32[]{:T(128)} %broadcast.497), dimensions={1}, to_apply=%all_to_all.22.reduce_sub_computation | reduce | bytes 2949124 | tf_op jit(solution)/shard_map/all_to_all | solution.py:37
  180.7 6.3 %reshape.790 = f32[5760,2,32]{2,1,0:T(2,128)} reshape(f32[64,5760]{1,0:T(8,128)S(1)} %reduce.2) | data formatting | bytes 2949120
  187.0 7.2 %copy.279 = f32[32,2,64,90]{3,0,1,2:T(8,128)S(1)} copy(f32[32,2,64,90]{0,1,3,2:T(2,128)} %bitcast.441) | data formatting | bytes 2949120 | tf_op jit(solution)/shard_map/all_to_all | solution.py:37
  199.6 3.0 %convolution_bitcast_fusion.8 = f32[5,8,128,90]{3,2,1,0:T(8,128)} fusion(f32[5,8,128,90]{3,2,1,0:T(8,128)S(1)} %multiply_dynamic-update-slice_fusion.2, s32[128]{0:T(128)S(1)} %copy-done.38), kind=kOutput, calls=%fused_computation.10 | convolution fusion | flops 707805184 | bytes 3686912 | tf_op jit(solution)/shard_map/ks,frsc->frkc/dot_general | solution.py:83
  202.6 3.0 %convolution_bitcast_fusion.6 = f32[5,8,128,90]{3,2,1,0:T(8,128)} fusion(f32[5,8,128,90]{3,2,1,0:T(8,128)S(1)} %multiply_dynamic-update-slice_fusion.2, s32[128]{0:T(128)S(1)} %copy-done.37), kind=kOutput, calls=%fused_computation.8 | convolution fusion | flops 707805184 | bytes 3686912 | tf_op jit(solution)/shard_map/ks,frsc->frkc/dot_general | solution.py:83
  210.7 2.3 collective-permute-start
  213.7 1.8 copy.309
  220.8 1.6 convolution_bitcast_fusion.4
  227.9 1.6 convolution_bitcast_fusion
  231.1 1.7 convolution_bitcast_fusion.2
  233.7 1.6 fusion.12
  235.4 1.6 fusion.36
  237.0 1.6 fusion.60
  238.9 2.6 copy.325
  241.4 10.5 %all-to-all-start.1 = ((f32[32,128,90]{2,0,1:T(8,128)}), f32[32,128,90]{2,0,1:T(8,128)S(1)}, u32[]{:S(2)}, u32[]{:S(2)}) async-start(f32[32,128,90]{2,0,1:T(8,128)} %copy.325), calls=%async_computation.1 | async-start | bytes 4194304 | tf_op jit(solution)/shard_map/all_to_all | solution.py:37
  251.9 1.6 fusion.122
  253.6 1.5 reduce_window_sum.22
  256.1 24.1 %all-to-all-done.1 = f32[32,128,90]{2,0,1:T(8,128)S(1)} async-done(((f32[32,128,90]{2,0,1:T(8,128)}), f32[32,128,90]{2,0,1:T(8,128)S(1)}, u32[]{:S(2)}, u32[]{:S(2)}) %all-to-all-start.1) | async-done | bytes 1474592 | tf_op jit(solution)/shard_map/all_to_all | solution.py:37
  (162 shorter events, 40.0 us)
Async XLA Ops:
  0.6 7.0 %copy-start.9 = (f32[8,2,5760]{2,1,0:T(2,128)S(1)}, f32[8,2,5760]{2,1,0:T(2,128)}, u32[]{:S(2)}) copy-start(f32[8,2,5760]{2,1,0:T(2,128)} %param.8) | copy-start | bytes 1105924
  7.6 5.5 %copy-start.14 = (f32[8,2,5760]{2,1,0:T(2,128)S(1)}, f32[8,2,5760]{2,1,0:T(2,128)}, u32[]{:S(2)}) copy-start(f32[8,2,5760]{2,1,0:T(2,128)} %param.9) | copy-start | bytes 1105924
  13.1 5.5 %copy-start.15 = (f32[8,2,5760]{2,1,0:T(2,128)S(1)}, f32[8,2,5760]{2,1,0:T(2,128)}, u32[]{:S(2)}) copy-start(f32[8,2,5760]{2,1,0:T(2,128)} %param.10) | copy-start | bytes 1105924
  54.1 11.7 %copy-start.21 = (s32[3,2,128,1,1]{2,4,3,1,0:T(1,128)S(1)}, s32[3,2,128,1,1]{2,4,3,1,0:T(1,128)}, u32[]{:S(2)}) copy-start(s32[3,2,128,1,1]{2,4,3,1,0:T(1,128)} %param.13) | copy-start | bytes 9220
  54.1 15.6 %copy-start.40 = (f32[129]{0:T(256)S(1)}, f32[129]{0:T(256)}, u32[]{:S(2)}) copy-start(f32[129]{0:T(256)} %param.12) | copy-start | bytes 1552
  54.1 121.9 %all-to-all-start = ((f32[64,1,5760]{2,1,0:T(1,128)}), f32[64,1,5760]{2,1,0:T(1,128)S(1)}, u32[]{:S(2)}, u32[]{:S(2)}) async-start(f32[64,1,5760]{2,1,0:T(1,128)} %reshape.789), calls=%async_computation | async-start | bytes 2949120 | tf_op jit(solution)/shard_map/all_to_all | solution.py:37
  69.8 136.5 %copy-start.19 = (f32[128]{0:T(128)}, f32[128]{0:T(128)S(1)}, u32[]{:S(2)}) copy-start(f32[128]{0:T(128)S(1)} %slice_subtract_fusion.2) | copy-start | bytes 1540
  107.9 14.9 %copy-start.13 = (f32[8,2,5760]{2,1,0:T(2,128)S(1)}, f32[8,2,5760]{2,1,0:T(2,128)}, u32[]{:S(2)}) copy-start(f32[8,2,5760]{2,1,0:T(2,128)} %param.7) | copy-start | bytes 1105924
  194.4 14.2 %copy-start.4 = (f32[8,64,2,90]{3,0,2,1:T(8,128)}, f32[8,64,2,90]{3,0,2,1:T(8,128)S(1)}, u32[]{:S(2)}) copy-start(f32[8,64,2,90]{3,0,2,1:T(8,128)S(1)} %get-tuple-element.15) | copy-start | bytes 1105924
  194.4 15.3 %copy-start.2 = (f32[8,64,2,90]{3,0,2,1:T(8,128)}, f32[8,64,2,90]{3,0,2,1:T(8,128)S(1)}, u32[]{:S(2)}) copy-start(f32[8,64,2,90]{3,0,2,1:T(8,128)S(1)} %get-tuple-element.14) | copy-start | bytes 1105924
  195.9 17.1 %collective-permute-start.1 = (f32[8,128]{1,0:T(8,128)S(1)}, f32[8,128]{1,0:T(8,128)S(1)}, u32[]{:S(2)}, u32[]{:S(2)}) collective-permute-start(f32[8,128]{1,0:T(8,128)S(1)} %slice_reduce_fusion), channel_id=1, source_target_pairs={{63,0},{0,1},{1,2},{2,3},{3,4},{4,5},{5,6},{6,7},{7,8},{8,9},{9,10... | collective-permute-start | bytes 12296 | tf_op jit(solution)/shard_map/ppermute | solution.py:50
  199.6 3.1 %copy-start.37 = (s32[128]{0:T(128)S(1)}, s32[128]{0:T(128)}, u32[]{:S(2)}) copy-start(s32[128]{0:T(128)} %get-tuple-element.46) | copy-start | bytes 1540
  210.7 4.8 %collective-permute-start = (f32[128,90]{1,0:T(8,128)}, f32[128,90]{1,0:T(8,128)}, u32[]{:S(2)}, u32[]{:S(2)}) collective-permute-start(f32[128,90]{1,0:T(8,128)} %slice_bitcast_fusion.36), channel_id=1, source_target_pairs={{0,64},{1,65},{2,66},{3,67},{4,68},{5,69},{6,70},{7,71},{8,72},{9,... | collective-permute-start | bytes 138248 | tf_op jit(solution)/shard_map/ppermute | solution.py:44
  218.1 1.6 copy-start.16
  220.8 1.6 copy-start.35
  227.9 1.6 copy-start.32
  231.1 1.8 copy-start.41
  231.1 2.0 copy-start
  231.1 2.5 copy-start.1
  231.1 2.5 copy-start.20
  231.1 2.5 copy-start.28
  231.1 2.5 copy-start.29
  231.1 2.5 copy-start.30
  233.6 1.7 copy-start.25
  233.6 1.7 copy-start.26
  233.6 1.7 copy-start.27
  235.3 1.7 copy-start.22
  235.3 1.7 copy-start.23
  235.3 1.7 copy-start.24
  237.0 1.7 copy-start.12
  241.4 10.5 %copy-start.7 = (f32[32,5760]{1,0:T(8,128)S(1)}, f32[32,5760]{1,0:T(8,128)}, u32[]{:S(2)}) copy-start(f32[32,5760]{1,0:T(8,128)} %copy-done.6) | copy-start | bytes 2211844
  241.4 38.8 %all-to-all-start.1 = ((f32[32,128,90]{2,0,1:T(8,128)}), f32[32,128,90]{2,0,1:T(8,128)S(1)}, u32[]{:S(2)}, u32[]{:S(2)}) async-start(f32[32,128,90]{2,0,1:T(8,128)} %copy.325), calls=%async_computation.1 | async-start | bytes 4194304 | tf_op jit(solution)/shard_map/all_to_all | solution.py:37
  (14 other events, 15.0 us)
where the time goes:
time: 293 us; the launch traced here: 289 us
  blocking collectives  103 us (35%)
  local copies, waits for them, and re-layouts  71.9 us (25%)
  other arithmetic  46.4 us (16%)
  starting transfers between devices  24.6 us (8%)
  waiting for transfers between devices  24.1 us (8%)
  matrix products  17.5 us (6%)
    all_gather x6, blocking collectives, carried_in(): pieces = lax.all_gather(running, axis)  103 us
    unnamed x97, local copies, waits for them, and re-layouts  43.8 us
    all_to_all x2, waiting for transfers between devices, side_by_side(): lax.all_to_all(both, axis, split_axis=split_dim, concat_axis=concat_dim,...  24.1 us
    all_to_all x2, starting transfers between devices, side_by_side(): lax.all_to_all(both, axis, split_axis=split_dim, concat_axis=concat_dim,...  22.2 us
    unnamed x6, other arithmetic  22.1 us
    dot_general x9, matrix products, remap_block(): jnp.einsum('ks,frsc->frkc', picker, stacked, precision=lax.Precision.HIGH...  17.1 us
    split x13, local copies, waits for them, and re-layouts, side_by_side(): jnp.split(whole, [sum(widths[:k]) for k in range(1, len(widths))], axis=a...  11.1 us
    all_to_all x2, local copies, waits for them, and re-layouts, side_by_side(): lax.all_to_all(both, axis, split_axis=split_dim, concat_axis=concat_dim,...  7.68 us
  transfers between devices with their start and end apart: 4, of which 1 were waited for; matrix products, arithmetic and copies ran while one was open for 9% of the time, Pallas kernels for 0%

commit v1 on v0

v1 whole, which is shorter than its diff:
```python
import functools

import jax
import jax.numpy as jnp
from jax import lax
from jax.experimental import pallas as pl
from jax.experimental.pallas import tpu as pltpu
from jax.sharding import PartitionSpec as P

TOP = 0.2
KAPPA = 0.2857
LEV = 128
LON = 5760
BLK = 90
N = 64
CHUNKS = LON // 128
STRIDE = 2 * CHUNKS
F32 = jnp.float32

FWD = ((1, 0, 0), (1, 1, 91), (0, 0, 182), (0, 1, 272), (2, 0, 384), (2, 1, 474), (3, 0, 564), (3, 1, 654))
FWD_REGS = 6
BACK = ((0, 0, 0), (0, 1, 90), (1, 0, 180), (2, 0, 270), (2, 1, 360), (3, 0, 450), (3, 1, 540), (4, 0, 630), (4, 1, 720))
BACK_REGS = 7


def lanes():
    return lax.broadcasted_iota(jnp.int32, (8, 128), 1)


def roll_lanes(x, shift):
    shift = shift % 128
    return x if shift == 0 else pltpu.roll(x, shift, axis=1)


def place(regs, piece, offset, width, lane):
    reg, start = divmod(offset, 128)
    regs[reg] = piece if regs[reg] is None else jnp.where(lane >= start, piece, regs[reg])
    if start + width > 128:
        regs[reg + 1] = piece


def take(load, offset, width, lane):
    reg, start = divmod(offset, 128)
    x = load(reg)
    if start + width > 128:
        x = jnp.where(lane >= start, x, load(reg + 1))
    return x


def pack_kernel(temp_ref, depth_ref, zonal_ref, merid_ref, out_ref):
    refs = (temp_ref, depth_ref, zonal_ref, merid_ref)
    lane = lanes()
    for c in range(N):
        regs = [None] * FWD_REGS
        for field, level, offset in FWD:
            extra = 1 if field == 1 else 0
            width = BLK + extra
            first = (BLK * c - extra) % LON
            chunk, start = divmod(first, 128)
            ref = refs[field]
            x = ref[pl.ds(2 * chunk + level, 8, stride=STRIDE), :]
            if start + width > 128:
                after = (chunk + 1) % CHUNKS
                y = ref[pl.ds(2 * after + level, 8, stride=STRIDE), :]
                x = jnp.where(lane >= start, x, y)
            place(regs, roll_lanes(x, offset - start), offset, width, lane)
        for r in range(FWD_REGS):
            out_ref[c, :, 128 * r : 128 * (r + 1)] = regs[r]


def compute_kernel(
    eta_ref, table_ref, recv_ref, partner_ref, out_ref,
    edge_ref, q_ref, rh_ref, c1_ref, c2_ref, c3_ref, res_ref,
):
    lane = lanes()
    row = lax.broadcasted_iota(jnp.int32, (8, 128), 0)
    lat = lax.axis_index("lat")
    own_first = jnp.logical_and(row == 0, lat == 0)
    top = jnp.full((8, 128), TOP, F32)
    for kind in range(3):
        edge_ref[kind, 0] = top

    def gather(s, carry):
        edge, south = carry

        def load(r):
            return recv_ref[s, :, 128 * r : 128 * (r + 1)]

        def load_south(r):
            theirs = partner_ref[s, :, 128 * r : 128 * (r + 1)]
            return jnp.where(row == 7, theirs, load(r))

        for field, level, offset in FWD:
            if field != 1:
                x = roll_lanes(take(load, offset, BLK, lane), -offset)
                q_ref[(0, 0, 1, 2)[field], 2 * s + level] = x
                continue
            x = roll_lanes(take(load, offset, BLK + 1, lane), -(offset + 1))
            y = roll_lanes(take(load_south, offset, BLK + 1, lane), -(offset + 1))
            y = jnp.where(own_first, x, pltpu.roll(y, 1, axis=0))
            edge = edge + x
            south = south + y
            at = 2 * s + level + 1
            edge_ref[0, at] = edge
            edge_ref[1, at] = 0.5 * (south + edge)
            edge_ref[2, at] = 0.5 * (roll_lanes(edge, 1) + edge)
        return edge, south

    last, _ = lax.fori_loop(0, N, gather, (top, top), unroll=2)

    def power(x):
        return jnp.exp(KAPPA * jnp.log(x))

    def integrate(t, carry):
        below, phi = carry
        s = LEV - 1 - t
        above = power(edge_ref[0, s])
        phi = phi + q_ref[0, s] * (below - above)
        res_ref[0, s] = phi
        return above, phi

    lax.fori_loop(0, LEV, integrate, (power(last), jnp.zeros((8, 128), F32)), unroll=4)

    for kind in range(3):

        def coefficients(s, left, right, q, edge, h):
            bend = q - 0.5 * (left + right)
            rh_ref[s] = 1.0 / h
            c1_ref[s] = h * left
            c2_ref[s] = h * (0.5 * (right - left) + 3.0 * bend)
            c3_ref[s] = -2.0 * (h * bend)

        def layer(s, carry):
            left, q, edge, h = carry
            lower = edge_ref[kind, s + 1]
            h_next = edge_ref[kind, s + 2] - lower
            q_next = q_ref[kind, s + 1]
            right = (h_next * q + h * q_next) / (h + h_next)
            coefficients(s, left, right, q, edge, h)
            return right, q_next, lower, h_next

        q0 = q_ref[kind, 0]
        h0 = edge_ref[kind, 1] - top
        left, q, edge, h = lax.fori_loop(0, LEV - 1, layer, (q0, q0, top, h0), unroll=4)
        coefficients(LEV - 1, left, q, q, edge, h)
        span = edge_ref[kind, LEV] - TOP

        def target(k, carry):
            upper = carry
            eta0, eta1 = eta_ref[k], eta_ref[k + 1]
            lower = TOP + eta1 * span
            start = table_ref[kind, 0, k]
            count = table_ref[kind, 1, k]
            total = jnp.zeros((8, 128), F32)
            for m in range(3):
                s = jnp.clip(start + m, 0, LEV - 1)
                weight = jnp.where(m < count, 1.0, 0.0).astype(F32)
                edge, rh = edge_ref[kind, s], rh_ref[s]
                c1, c2, c3 = c1_ref[s], c2_ref[s], c3_ref[s]
                x1 = jnp.clip((upper - edge) * rh, 0.0, 1.0)
                x2 = jnp.clip((lower - edge) * rh, 0.0, 1.0)
                share = x2 * (c1 + x2 * (c2 + x2 * c3)) - x1 * (c1 + x1 * (c2 + x1 * c3))
                total = total + weight * share
            res_ref[2 + kind, k] = total / ((eta1 - eta0) * span)
            return lower

        lax.fori_loop(0, LEV, target, TOP + eta_ref[0] * span, unroll=4)

    span = last - TOP

    def send(s, _):
        regs = [None] * BACK_REGS
        for field, level, offset in BACK:
            x = span if field == 1 else res_ref[field, 2 * s + level]
            place(regs, roll_lanes(x, offset), offset, BLK, lane)
        for r in range(BACK_REGS):
            out_ref[s, :, 128 * r : 128 * (r + 1)] = regs[r]
        return 0

    lax.fori_loop(0, N, send, 0, unroll=2)


def unpack_kernel(eta_ref, recv_ref, surface_ref, temp_ref, depth_ref, zonal_ref, merid_ref, phi_ref):
    lane = lanes()
    me = lax.axis_index("lev")
    steps = [eta_ref[2 * me + level + 1] - eta_ref[2 * me + level] for level in range(2)]
    for field, level, offset in BACK:
        current = None
        for c in range(N):

            def load(r):
                return recv_ref[c, :, 128 * r : 128 * (r + 1)]

            chunk, start = divmod(BLK * c, 128)
            x = roll_lanes(take(load, offset, BLK, lane), start - offset)
            current = x if start == 0 else jnp.where(lane >= start, x, current)
            if start + BLK < 128:
                continue
            if field == 1:
                for k in range(2):
                    depth_ref[pl.ds(2 * chunk + k, 8, stride=STRIDE), :] = steps[k] * current
            else:
                y = current
                if field == 0:
                    y = y + surface_ref[:, 128 * chunk : 128 * (chunk + 1)]
                ref = (phi_ref, None, temp_ref, zonal_ref, merid_ref)[field]
                ref[pl.ds(2 * chunk + level, 8, stride=STRIDE), :] = y
            current = x


def to_rows(x):
    return x.reshape(8, 2, CHUNKS, 128).transpose(0, 2, 1, 3).reshape(8 * STRIDE, 128)


def from_rows(x):
    return x.reshape(8, CHUNKS, 2, 128).transpose(0, 2, 1, 3).reshape(8, 2, LON)


VMEM = pl.BlockSpec(memory_space=pltpu.VMEM)
SMEM = pl.BlockSpec(memory_space=pltpu.SMEM)


def on_device(temp, depth, zonal, merid, surface, eta, intersection):
    table = intersection[:, :, :, 0, 0]
    packed = pl.pallas_call(
        pack_kernel,
        out_shape=jax.ShapeDtypeStruct((N, 8, 128 * FWD_REGS), F32),
        in_specs=[VMEM] * 4,
        out_specs=VMEM,
        name="pack",
    )(*(to_rows(x) for x in (temp, depth, zonal, merid)))
    recv = lax.all_to_all(packed, "lev", 0, 0, tiled=True)
    partner = lax.ppermute(recv[:, :, :256], "lat", [(0, 1), (1, 0)])
    block = pltpu.VMEM((LEV, 8, 128), F32)
    out = pl.pallas_call(
        compute_kernel,
        out_shape=jax.ShapeDtypeStruct((N, 8, 128 * BACK_REGS), F32),
        in_specs=[SMEM, SMEM, VMEM, VMEM],
        out_specs=VMEM,
        scratch_shapes=[
            pltpu.VMEM((3, LEV + 1, 8, 128), F32),
            pltpu.VMEM((3, LEV, 8, 128), F32),
            block, block, block, block,
            pltpu.VMEM((5, LEV, 8, 128), F32),
        ],
        name="remap",
    )(eta, table, recv, partner)
    back = lax.all_to_all(out, "lev", 0, 0, tiled=True)
    outs = pl.pallas_call(
        unpack_kernel,
        out_shape=[jax.ShapeDtypeStruct((8 * STRIDE, 128), F32)] * 5,
        in_specs=[SMEM, VMEM, VMEM],
        out_specs=[VMEM] * 5,
        name="unpack",
    )(eta, back, surface)
    return tuple(from_rows(x) for x in outs)


def solution(mesh):
    shards = P("lat", "lev", None)
    return jax.shard_map(
        on_device,
        mesh=mesh,
        in_specs=(shards,) * 4 + (P("lat", None), P(), P(None, None, None, "lat", "lev")),
        out_specs=(shards,) * 5,
        check_vma=False,
    )
```

time: 293 us -> 112 us (0.38); the launches traced: 289 us -> 112 us
  local copies, waits for them, and re-layouts: 71.9 us -> 13.9 us
  other arithmetic: 46.4 us -> 0 us
  blocking collectives: 103 us -> 69.3 us
  Pallas kernels: 0 us -> 25.9 us
  starting transfers between devices: 24.6 us -> 0.09 us
  waiting for transfers between devices: 24.1 us -> 1.9 us
  matrix products: 17.5 us -> 0 us
    all_gather x6 -> x0, blocking collectives: 103 us -> none  [carried_in(): pieces = lax.all_gather(running, axis)]
    all_to_all x0 -> x2, blocking collectives: none -> 69.3 us  [the longest x1 35.9 us: on_device(): recv = lax.all_to_all(packed, 'lev', 0, 0, tiled=True)]
    unnamed x97 -> x21, local copies, waits for them, and re-layouts: 43.8 us -> 5.46 us
    pallas_call x0 -> x3, Pallas kernels: none -> 25.9 us  [the longest x1 19.5 us: on_device(): pl.pallas_call(compute_kernel, out_shape=jax.ShapeDtypeStruct((N, 8, 128...]
    all_to_all x2 -> x0, waiting for transfers between devices: 24.1 us -> none  [side_by_side(): lax.all_to_all(both, axis, split_axis=split_dim, concat_axis=concat_dim,...]
    all_to_all x2 -> x0, starting transfers between devices: 22.2 us -> none  [side_by_side(): lax.all_to_all(both, axis, split_axis=split_dim, concat_axis=concat_dim,...]
    unnamed x6 -> x0, other arithmetic: 22.1 us -> none
    dot_general x10 -> x0, matrix products: 17.5 us -> none  [the longest x9 17.1 us: remap_block(): jnp.einsum('ks,frsc->frkc', picker, stacked, precision=lax.Precision.HIGH...]
  transfers between devices with their start and end apart: 4 -> 1, of which waited for: 1 -> 1; matrix products, arithmetic and copies ran while one was open for 9% -> 0% of each run, Pallas kernels for 0% -> 0%
where the time goes in v1:
time: 112 us
  blocking collectives  69.3 us (62%)
  Pallas kernels  25.9 us (23%)
  local copies, waits for them, and re-layouts  13.9 us (12%)
  waiting for transfers between devices  1.9 us (2%)
    all_to_all x1, blocking collectives, on_device(): recv = lax.all_to_all(packed, 'lev', 0, 0, tiled=True)  35.9 us
    all_to_all x1, blocking collectives, on_device(): back = lax.all_to_all(out, 'lev', 0, 0, tiled=True)  33.3 us
    pallas_call x1, Pallas kernels, on_device(): pl.pallas_call(compute_kernel, out_shape=jax.ShapeDtypeStruct((N, 8, 128...  19.5 us
    unnamed x21, local copies, waits for them, and re-layouts  5.46 us
    transpose x4, local copies, waits for them, and re-layouts, to_rows(): x.reshape(8, 2, CHUNKS, 128).transpose(0, 2, 1, 3).reshape(8 * STRIDE, 128)  3.71 us
    pallas_call x1, Pallas kernels, on_device(): pl.pallas_call(unpack_kernel, out_shape=[jax.ShapeDtypeStruct((8 * STRIDE...  3.3 us
    reshape x4, local copies, waits for them, and re-layouts, to_rows(): x.reshape(8, 2, CHUNKS, 128).transpose(0, 2, 1, 3).reshape(8 * STRIDE, 128)  3.2 us
    pallas_call x1, Pallas kernels, on_device(): pl.pallas_call(pack_kernel, out_shape=jax.ShapeDtypeStruct((N, 8, 128 * F...  3.07 us
  transfers between devices with their start and end apart: 1, of which 1 were waited for; matrix products, arithmetic and copies ran while one was open for 0% of the time, Pallas kernels for 0%

profile of v1, /device:TPU:0, one launch (start us, length us, event | category | flops | bytes accessed | tf_op | source)
XLA Modules:
  0.0 111.8 jit_solution(9158591719820944165)
XLA Ops:
  0.6 0.0 copy-start.2
  0.6 1.3 %reshape.82 = f32[8,2,45,128]{3,2,1,0:T(8,128)S(1)} reshape(f32[8,2,5760]{2,1,0:T(2,128)} %param.7) | data formatting | bytes 737280 | tf_op jit(solution)/shard_map/reshape | solution.py:212
  2.0 0.0 copy-start.3
  2.0 0.9 copy.22
  2.9 1.3 %reshape.83 = f32[8,2,45,128]{3,2,1,0:T(8,128)S(1)} reshape(f32[8,2,5760]{2,1,0:T(2,128)} %param.8) | data formatting | bytes 737280 | tf_op jit(solution)/shard_map/reshape | solution.py:212
  4.2 0.9 copy.24
  5.1 0.0 copy-done.2
  5.1 0.3 reshape.84
  5.4 0.9 copy.26
  6.4 0.3 reshape.85
  6.7 0.9 copy.28
  7.6 3.1 %pack.1 = f32[64,8,768]{2,1,0:T(8,128)} custom-call(f32[720,128]{1,0:T(8,128)} %bitcast.52, f32[720,128]{1,0:T(8,128)} %bitcast.53, f32[720,128]{1,0:T(8,128)} %bitcast.54, f32[720,128]{1,0:T(8,128)} %bitcast.55), custom_call_target="tpu_custom_call" | custom-call | tf_op jit(solution)/shard_map/pack/pallas_call | solution.py:225
  10.7 35.9 %all_to_all.10.recv_ref = f32[64,8,768]{2,1,0:T(8,128)S(1)} all-to-all(f32[64,8,768]{2,1,0:T(8,128)} %pack.1), channel_id=1, replica_groups=mesh['lat'=2,'lev'=64] {'lev'}, dimensions={0} | all-to-all | bytes 3145728 | tf_op jit(solution)/shard_map/all_to_all | solution.py:232
  46.6 0.1 collective-permute-start
  46.7 1.9 %collective-permute-done.partner_ref = f32[64,8,256]{2,1,0:T(8,128)S(1)} collective-permute-done((f32[64,8,256]{2,1,0:T(8,128)S(1)}, f32[64,8,256]{2,1,0:T(8,128)S(1)}, u32[]{:S(2)}, u32[]{:S(2)}) %collective-permute-start) | collective-permute-done | bytes 524320 | tf_op jit(solution)/shard_map/ppermute | solution.py:233
  48.6 0.0 copy-done
  48.6 0.8 copy-done.1
  49.4 19.5 %remap.1 = f32[64,8,896]{2,1,0:T(8,128)} custom-call(f32[129]{0:T(256)} %eta_ref.3, s32[3,2,128]{2,1,0:T(2,128)} %bitcast.61, f32[64,8,768]{2,1,0:T(8,128)} %copy-done, f32[64,8,256]{2,1,0:T(8,128)} %copy-done.1), custom_call_target="tpu_custom_call" | custom-call | tf_op jit(solution)/shard_map/remap/pallas_call | solution.py:235
  68.9 33.3 %all_to_all.11.recv_ref = f32[64,8,896]{2,1,0:T(8,128)} all-to-all(f32[64,8,896]{2,1,0:T(8,128)} %remap.1), channel_id=1, replica_groups=mesh['lat'=2,'lev'=64] {'lev'}, dimensions={0} | all-to-all | bytes 3670016 | tf_op jit(solution)/shard_map/all_to_all | solution.py:248
  102.3 3.3 %unpack.1 = (f32[720,128]{1,0:T(8,128)}, f32[720,128]{1,0:T(8,128)}, f32[720,128]{1,0:T(8,128)}, f32[720,128]{1,0:T(8,128)}, f32[720,128]{1,0:T(8,128)}) custom-call(f32[129]{0:T(256)} %eta_ref.3, f32[64,8,896]{2,1,0:T(8,128)} %all_to_all.11.recv_ref, f32[8,5760]{1,0:T(8,128)} %surface_ref.1), custom_call_target="tpu_custom_call" | custom-call | tf_op jit(solution)/shard_map/unpack/pallas_call | solution.py:249
  105.6 1.1 copy.55
  106.6 0.0 copy-start.6
  106.6 0.1 reshape.75
  106.7 0.9 copy.35
  107.7 0.1 reshape.73
  107.7 0.9 copy.34
  108.7 0.1 reshape.77
  108.8 0.9 copy.36
  109.7 0.1 reshape.79
  109.8 0.9 copy.37
  110.8 0.1 reshape.81
  110.8 0.9 copy.38
  (15 shorter events, 0.2 us)
Async XLA Ops:
  0.6 4.5 %copy-start.2 = (f32[8,2,5760]{2,1,0:T(2,128)S(1)}, f32[8,2,5760]{2,1,0:T(2,128)}, u32[]{:S(2)}) copy-start(f32[8,2,5760]{2,1,0:T(2,128)} %param.9) | copy-start | bytes 1105924
  2.0 4.4 %copy-start.3 = (f32[8,2,5760]{2,1,0:T(2,128)S(1)}, f32[8,2,5760]{2,1,0:T(2,128)}, u32[]{:S(2)}) copy-start(f32[8,2,5760]{2,1,0:T(2,128)} %param.10) | copy-start | bytes 1105924
  46.6 2.0 %copy-start = (f32[64,8,768]{2,1,0:T(8,128)}, f32[64,8,768]{2,1,0:T(8,128)S(1)}, u32[]{:S(2)}) copy-start(f32[64,8,768]{2,1,0:T(8,128)S(1)} %all_to_all.10.recv_ref) | copy-start | bytes 4718596
  46.6 2.0 %collective-permute-start = (f32[64,8,256]{2,1,0:T(8,128)S(1)}, f32[64,8,256]{2,1,0:T(8,128)S(1)}, u32[]{:S(2)}, u32[]{:S(2)}) collective-permute-start(f32[64,8,256]{2,1,0:T(8,128)S(1)} %slice.4), channel_id=1, source_target_pairs={{0,64},{64,0},{1,65},{65,1},{2,66},{66,2},{3,67},{67,3},{4,68},{68... | collective-permute-start | bytes 1572872 | tf_op jit(solution)/shard_map/ppermute | solution.py:233
  48.6 0.8 copy-start.1
  105.5 2.1 %copy-start.7 = (f32[720,128]{1,0:T(8,128)S(1)}, f32[720,128]{1,0:T(8,128)}, u32[]{:S(2)}) copy-start(f32[720,128]{1,0:T(8,128)} %get-tuple-element.10) | copy-start | bytes 1105924
  106.6 2.0 %copy-start.6 = (f32[720,128]{1,0:T(8,128)S(1)}, f32[720,128]{1,0:T(8,128)}, u32[]{:S(2)}) copy-start(f32[720,128]{1,0:T(8,128)} %get-tuple-element.12) | copy-start | bytes 1105924
  107.7 2.0 %copy-start.5 = (f32[720,128]{1,0:T(8,128)S(1)}, f32[720,128]{1,0:T(8,128)}, u32[]{:S(2)}) copy-start(f32[720,128]{1,0:T(8,128)} %get-tuple-element.13) | copy-start | bytes 1105924
  108.7 2.0 %copy-start.4 = (f32[720,128]{1,0:T(8,128)S(1)}, f32[720,128]{1,0:T(8,128)}, u32[]{:S(2)}) copy-start(f32[720,128]{1,0:T(8,128)} %get-tuple-element.14) | copy-start | bytes 1105924

commit v2 on v1

--- a/solution.py
+++ b/solution.py
@@ -14,7 +14,6 @@
 BLK = 90
 N = 64
 CHUNKS = LON // 128
-STRIDE = 2 * CHUNKS
 F32 = jnp.float32
 
 FWD = ((1, 0, 0), (1, 1, 91), (0, 0, 182), (0, 1, 272), (2, 0, 384), (2, 1, 474), (3, 0, 564), (3, 1, 654))
@@ -58,10 +57,10 @@
             first = (BLK * c - extra) % LON
             chunk, start = divmod(first, 128)
             ref = refs[field]
-            x = ref[pl.ds(2 * chunk + level, 8, stride=STRIDE), :]
+            x = ref[:, level, 128 * chunk : 128 * (chunk + 1)]
             if start + width > 128:
                 after = (chunk + 1) % CHUNKS
-                y = ref[pl.ds(2 * after + level, 8, stride=STRIDE), :]
+                y = ref[:, level, 128 * after : 128 * (after + 1)]
                 x = jnp.where(lane >= start, x, y)
             place(regs, roll_lanes(x, offset - start), offset, width, lane)
         for r in range(FWD_REGS):
@@ -198,22 +197,14 @@
                 continue
             if field == 1:
                 for k in range(2):
-                    depth_ref[pl.ds(2 * chunk + k, 8, stride=STRIDE), :] = steps[k] * current
+                    depth_ref[:, k, 128 * chunk : 128 * (chunk + 1)] = steps[k] * current
             else:
                 y = current
                 if field == 0:
                     y = y + surface_ref[:, 128 * chunk : 128 * (chunk + 1)]
                 ref = (phi_ref, None, temp_ref, zonal_ref, merid_ref)[field]
-                ref[pl.ds(2 * chunk + level, 8, stride=STRIDE), :] = y
+                ref[:, level, 128 * chunk : 128 * (chunk + 1)] = y
             current = x
-
-
-def to_rows(x):
-    return x.reshape(8, 2, CHUNKS, 128).transpose(0, 2, 1, 3).reshape(8 * STRIDE, 128)
-
-
-def from_rows(x):
-    return x.reshape(8, CHUNKS, 2, 128).transpose(0, 2, 1, 3).reshape(8, 2, LON)
 
 
 VMEM = pl.BlockSpec(memory_space=pltpu.VMEM)
@@ -228,7 +219,7 @@
         in_specs=[VMEM] * 4,
         out_specs=VMEM,
         name="pack",
-    )(*(to_rows(x) for x in (temp, depth, zonal, merid)))
+    )(temp, depth, zonal, merid)
     recv = lax.all_to_all(packed, "lev", 0, 0, tiled=True)
     partner = lax.ppermute(recv[:, :, :256], "lat", [(0, 1), (1, 0)])
     block = pltpu.VMEM((LEV, 8, 128), F32)
@@ -248,12 +239,12 @@
     back = lax.all_to_all(out, "lev", 0, 0, tiled=True)
     outs = pl.pallas_call(
         unpack_kernel,
-        out_shape=[jax.ShapeDtypeStruct((8 * STRIDE, 128), F32)] * 5,
+        out_shape=[jax.ShapeDtypeStruct((8, 2, LON), F32)] * 5,
         in_specs=[SMEM, VMEM, VMEM],
         out_specs=[VMEM] * 5,
         name="unpack",
     )(eta, back, surface)
-    return tuple(from_rows(x) for x in outs)
+    return tuple(outs)
 
 
 def solution(mesh):

time: 112 us -> 101 us (0.902)
  local copies, waits for them, and re-layouts: 13.9 us -> 0.83 us
  Pallas kernels: 25.9 us -> 28.4 us
    reshape x14 -> x0, local copies, waits for them, and re-layouts: 4.68 us -> none  [the longest x4 3.2 us: to_rows(): x.reshape(8, 2, CHUNKS, 128).transpose(0, 2, 1, 3).reshape(8 * STRIDE, 128)]
    unnamed x21 -> x4, local copies, waits for them, and re-layouts: 5.46 us -> 0.8 us
    transpose x4 -> x0, local copies, waits for them, and re-layouts: 3.71 us -> none  [to_rows(): x.reshape(8, 2, CHUNKS, 128).transpose(0, 2, 1, 3).reshape(8 * STRIDE, 128)]
    pallas_call x1, Pallas kernels: 3.07 us -> 5.01 us  [on_device(): pl.pallas_call(pack_kernel, out_shape=jax.ShapeDtypeStruct((N, 8, 128 * F...]
where the time goes in v2:
time: 101 us
  blocking collectives  69.3 us (69%)
  Pallas kernels  28.4 us (28%)
  waiting for transfers between devices  1.9 us (2%)
    all_to_all x1, blocking collectives, on_device(): recv = lax.all_to_all(packed, 'lev', 0, 0, tiled=True)  35.9 us
    all_to_all x1, blocking collectives, on_device(): back = lax.all_to_all(out, 'lev', 0, 0, tiled=True)  33.3 us
    pallas_call x1, Pallas kernels, on_device(): pl.pallas_call(compute_kernel, out_shape=jax.ShapeDtypeStruct((N, 8, 128...  19.5 us
    pallas_call x1, Pallas kernels, on_device(): pl.pallas_call(pack_kernel, out_shape=jax.ShapeDtypeStruct((N, 8, 128 * F...  5.01 us
    pallas_call x1, Pallas kernels, on_device(): pl.pallas_call(unpack_kernel, out_shape=[jax.ShapeDtypeStruct((8, 2, LON)...  3.82 us
  transfers between devices with their start and end apart: 1, of which 1 were waited for; matrix products, arithmetic and copies ran while one was open for 0% of the time, Pallas kernels for 0%

profile of v2, /device:TPU:0, one launch (start us, length us, event | category | flops | bytes accessed | tf_op | source)
XLA Modules:
  0.0 101.1 jit_solution(12806700367669582930)
XLA Ops:
  0.6 5.0 %pack.1 = f32[64,8,768]{2,1,0:T(8,128)} custom-call(f32[8,2,5760]{2,1,0:T(2,128)} %temp_ref.1, f32[8,2,5760]{2,1,0:T(2,128)} %depth_ref.1, f32[8,2,5760]{2,1,0:T(2,128)} %zonal_ref.1, f32[8,2,5760]{2,1,0:T(2,128)} %merid_ref.1), custom_call_target="tpu_custom_call" | custom-call | tf_op jit(solution)/shard_map/pack/pallas_call | solution.py:216
  5.6 35.9 %all_to_all.10.recv_ref = f32[64,8,768]{2,1,0:T(8,128)S(1)} all-to-all(f32[64,8,768]{2,1,0:T(8,128)} %pack.1), channel_id=1, replica_groups=mesh['lat'=2,'lev'=64] {'lev'}, dimensions={0} | all-to-all | bytes 3145728 | tf_op jit(solution)/shard_map/all_to_all | solution.py:223
  41.6 0.0 copy-start
  41.6 0.1 collective-permute-start
  41.7 1.9 %collective-permute-done.partner_ref = f32[64,8,256]{2,1,0:T(8,128)S(1)} collective-permute-done((f32[64,8,256]{2,1,0:T(8,128)S(1)}, f32[64,8,256]{2,1,0:T(8,128)S(1)}, u32[]{:S(2)}, u32[]{:S(2)}) %collective-permute-start) | collective-permute-done | bytes 524320 | tf_op jit(solution)/shard_map/ppermute | solution.py:224
  43.6 0.0 copy-start.1
  43.6 0.0 copy-done
  43.6 0.8 copy-done.1
  44.4 19.5 %remap.1 = f32[64,8,896]{2,1,0:T(8,128)} custom-call(f32[129]{0:T(256)} %eta_ref.3, s32[3,2,128]{2,1,0:T(2,128)} %bitcast.1, f32[64,8,768]{2,1,0:T(8,128)} %copy-done, f32[64,8,256]{2,1,0:T(8,128)} %copy-done.1), custom_call_target="tpu_custom_call" | custom-call | tf_op jit(solution)/shard_map/remap/pallas_call | solution.py:226
  63.9 33.3 %all_to_all.11.recv_ref = f32[64,8,896]{2,1,0:T(8,128)} all-to-all(f32[64,8,896]{2,1,0:T(8,128)} %remap.1), channel_id=1, replica_groups=mesh['lat'=2,'lev'=64] {'lev'}, dimensions={0} | all-to-all | bytes 3670016 | tf_op jit(solution)/shard_map/all_to_all | solution.py:239
  97.3 3.8 %unpack.1 = (f32[8,2,5760]{2,1,0:T(2,128)}, f32[8,2,5760]{2,1,0:T(2,128)}, f32[8,2,5760]{2,1,0:T(2,128)}, f32[8,2,5760]{2,1,0:T(2,128)}, f32[8,2,5760]{2,1,0:T(2,128)}) custom-call(f32[129]{0:T(256)} %eta_ref.3, f32[64,8,896]{2,1,0:T(8,128)} %all_to_all.11.recv_ref, f32[8,5760]{1,0:T(8,128)} %surface_ref.1), custom_call_target="tpu_custom_call" | custom-call | tf_op jit(solution)/shard_map/unpack/pallas_call | solution.py:240
  (1 shorter events, 0.0 us)
Async XLA Ops:
  41.6 2.0 %copy-start = (f32[64,8,768]{2,1,0:T(8,128)}, f32[64,8,768]{2,1,0:T(8,128)S(1)}, u32[]{:S(2)}) copy-start(f32[64,8,768]{2,1,0:T(8,128)S(1)} %all_to_all.10.recv_ref) | copy-start | bytes 4718596
  41.6 2.0 %collective-permute-start = (f32[64,8,256]{2,1,0:T(8,128)S(1)}, f32[64,8,256]{2,1,0:T(8,128)S(1)}, u32[]{:S(2)}, u32[]{:S(2)}) collective-permute-start(f32[64,8,256]{2,1,0:T(8,128)S(1)} %slice.4), channel_id=1, source_target_pairs={{0,64},{64,0},{1,65},{65,1},{2,66},{66,2},{3,67},{67,3},{4,68},{68... | collective-permute-start | bytes 1572872 | tf_op jit(solution)/shard_map/ppermute | solution.py:224
  43.6 0.8 copy-start.1

commit v3 on v2

v3 whole, which is shorter than its diff:
```python
import functools

import jax
import jax.numpy as jnp
from jax import lax
from jax.experimental import pallas as pl
from jax.experimental.pallas import tpu as pltpu
from jax.sharding import PartitionSpec as P

TOP = 0.2
KAPPA = 0.2857
LEV = 128
LON = 5760
BLK = 90
N = 64
CHUNKS = LON // 128
F32 = jnp.float32

FWD_A = ((1, 0, 0), (1, 1, 91), (0, 0, 182), (0, 1, 272))
FWD_B = ((2, 0, 0), (2, 1, 90), (3, 0, 180), (3, 1, 270))
BACK_A = ((0, 0, 0), (0, 1, 90), (1, 0, 180), (1, 1, 270), (2, 0, 360))
BACK_B = ((3, 0, 0), (3, 1, 90), (4, 0, 180), (4, 1, 270))
REGS_F, REGS_A, REGS_B = 3, 4, 3
MESH = pl.DeviceIdType.MESH


def lanes():
    return lax.broadcasted_iota(jnp.int32, (8, 128), 1)


def roll_lanes(x, shift):
    shift = shift % 128
    return x if isinstance(shift, int) and shift == 0 else pltpu.roll(x, shift, axis=1)


def place(regs, piece, offset, width, lane):
    reg, start = divmod(offset, 128)
    regs[reg] = piece if regs[reg] is None else jnp.where(lane >= start, piece, regs[reg])
    if start + width > 128:
        regs[reg + 1] = piece


def take(load, offset, width, lane):
    reg, start = divmod(offset, 128)
    x = load(reg)
    if start + width > 128:
        x = jnp.where(lane >= start, x, load(reg + 1))
    return x


def main_kernel(
    eta_ref, table_ref, temp_ref, depth_ref, zonal_ref, merid_ref, back_a, back_b,
    send_a, send_b, land_a, land_b, south_ref, ret_a, ret_b,
    edge_ref, q_ref, par_ref, res_ref, send_sem, recv_sem, own_sem,
):
    lat, me = lax.axis_index("lat"), lax.axis_index("lev")
    lane = lanes()
    row = lax.broadcasted_iota(jnp.int32, (8, 128), 0)
    other = (1 - lat, me)

    def peer(k):
        o = lax.rem(27 * k, N)
        x = lax.rem(lax.rem(me, 4) + lax.rem(o, 4), 4)
        y = lax.rem(lax.rem(me // 4, 4) + lax.rem(o // 4, 4), 4)
        z = lax.rem(me // 16 + o // 16, 4)
        return 16 * z + 4 * y + x

    barrier = pltpu.get_barrier_semaphore()

    def greet(k, _):
        pl.semaphore_signal(barrier, inc=1, device_id=(lat, peer(k)), device_id_type=MESH)
        return 0

    lax.fori_loop(1, N, greet, 0)
    pl.semaphore_signal(barrier, inc=1, device_id=other, device_id_type=MESH)

    def copy(src, dst, i, device):
        return pltpu.make_async_remote_copy(
            src_ref=src, dst_ref=dst, send_sem=send_sem.at[i], recv_sem=recv_sem.at[i],
            device_id=device, device_id_type=MESH,
        )

    def scatter(src, dst, i):
        def start(k, _):
            p = peer(k)
            copy(src.at[p], dst.at[me], i, (lat, p)).start()
            return 0

        lax.fori_loop(1, N, start, 0)

    def everyone(src, dst, i):
        return copy(src.at[pl.ds(0, N - 1)], dst.at[pl.ds(0, N - 1)], i, other)

    refs = (temp_ref, depth_ref, zonal_ref, merid_ref)

    def pack(c, _):
        for pieces, out in ((FWD_A, send_a), (FWD_B, send_b)):
            regs = [None] * REGS_F
            for field, level, offset in pieces:
                extra = 1 if field == 1 else 0
                first = lax.rem(BLK * c - extra + LON, LON)
                chunk, start = first // 128, lax.rem(first, 128)
                after = lax.rem(chunk + 1, CHUNKS)
                x = refs[field][:, level, pl.ds(pl.multiple_of(128 * chunk, 128), 128)]
                y = refs[field][:, level, pl.ds(pl.multiple_of(128 * after, 128), 128)]
                x = jnp.where(lane >= start, x, y)
                x = pltpu.roll(x, lax.rem(offset % 128 - start + 128, 128), axis=1)
                place(regs, x, offset, BLK + extra, lane)
            for r in range(REGS_F):
                out[c, :, 128 * r : 128 * (r + 1)] = regs[r]
        return 0

    lax.fori_loop(0, N, pack, 0, unroll=2)
    pl.semaphore_wait(barrier, N)
    scatter(send_a, land_a, 0)
    scatter(send_b, land_b, 1)
    land_a[me] = send_a[me]
    land_b[me] = send_b[me]

    top = jnp.full((8, 128), TOP, F32)
    zero = jnp.zeros((8, 128), F32)
    for kind in range(3):
        edge_ref[kind, 0] = top
    for p in range(5):
        par_ref[LEV, p] = zero

    def piece(ref, s, offset, width, shift):
        def load(r):
            return ref[s, :, 128 * r : 128 * (r + 1)]

        return roll_lanes(take(load, offset, width, lane), shift - offset)

    everyone(send_a, land_a, 0).wait_recv()
    share = copy(land_a.at[:, :, pl.ds(0, 256)], south_ref, 4, other)
    share.start()

    def gather_a(s, edge):
        for field, level, offset in FWD_A:
            if field == 0:
                q_ref[0, 2 * s + level] = piece(land_a, s, offset, BLK, 0)
                continue
            edge = edge + piece(land_a, s, offset, BLK + 1, -1)
            at = 2 * s + level + 1
            edge_ref[0, at] = edge
            edge_ref[2, at] = 0.5 * (roll_lanes(edge, 1) + edge)
        return edge

    last = lax.fori_loop(0, N, gather_a, top, unroll=2)

    def power(x):
        return jnp.exp(KAPPA * jnp.log(x))

    def integrate(t, carry):
        below, phi = carry
        s = LEV - 1 - t
        above = power(edge_ref[0, s])
        phi = phi + q_ref[0, s] * (below - above)
        res_ref[0, s] = phi
        return above, phi

    lax.fori_loop(0, LEV, integrate, (power(last), zero), unroll=4)

    def remap(kind, slot):
        def coefficients(s, left, right, q, edge, h):
            bend = q - 0.5 * (left + right)
            par_ref[s, 0] = edge
            par_ref[s, 1] = 1.0 / h
            par_ref[s, 2] = h * left
            par_ref[s, 3] = h * (0.5 * (right - left) + 3.0 * bend)
            par_ref[s, 4] = -2.0 * (h * bend)

        def layer(s, carry):
            left, q, edge, h = carry
            lower = edge_ref[kind, s + 1]
            h_next = edge_ref[kind, s + 2] - lower
            q_next = q_ref[kind, s + 1]
            right = (h_next * q + h * q_next) / (h + h_next)
            coefficients(s, left, right, q, edge, h)
            return right, q_next, lower, h_next

        q0 = q_ref[kind, 0]
        h0 = edge_ref[kind, 1] - top
        left, q, edge, h = lax.fori_loop(0, LEV - 1, layer, (q0, q0, top, h0), unroll=4)
        coefficients(LEV - 1, left, q, q, edge, h)
        span = edge_ref[kind, LEV] - TOP

        def target(k, upper):
            eta0, eta1 = eta_ref[k], eta_ref[k + 1]
            lower = TOP + eta1 * span
            first = table_ref[kind, 0, k]
            count = table_ref[kind, 1, k]
            total = zero
            for m in range(3):
                s = jnp.where(m < count, first + m, LEV)
                edge, rh = par_ref[s, 0], par_ref[s, 1]
                c1, c2, c3 = par_ref[s, 2], par_ref[s, 3], par_ref[s, 4]
                x1 = jnp.clip((upper - edge) * rh, 0.0, 1.0)
                x2 = jnp.clip((lower - edge) * rh, 0.0, 1.0)
                total = total + (x2 * (c1 + x2 * (c2 + x2 * c3)) - x1 * (c1 + x1 * (c2 + x1 * c3)))
            res_ref[slot, k] = total / ((eta1 - eta0) * span)
            return lower

        lax.fori_loop(0, LEV, target, TOP + eta_ref[0] * span, unroll=4)

    def send_back(pieces, regs_of, out, span):
        def build(s, _):
            regs = [None] * regs_of
            for field, level, offset in pieces:
                x = span if field == 2 else res_ref[field, 2 * s + level]
                place(regs, roll_lanes(x, offset), offset, BLK, lane)
            for r in range(regs_of):
                out[s, :, 128 * r : 128 * (r + 1)] = regs[r]
            return 0

        lax.fori_loop(0, N, build, 0, unroll=2)

    remap(0, 1)
    send_back(BACK_A, REGS_A, ret_a, last - TOP)
    scatter(ret_a, back_a, 2)

    everyone(send_b, land_b, 1).wait_recv()
    share.wait_recv()
    own_first = jnp.logical_and(row == 0, lat == 0)

    def gather_b(s, south):
        for field, level, offset in FWD_B:
            q_ref[field - 1, 2 * s + level] = piece(land_b, s, offset, BLK, 0)
        for level, offset in ((0, 0), (1, 91)):
            south = south + piece(south_ref, s, offset, BLK + 1, -1)
            at = 2 * s + level + 1
            own = edge_ref[0, at]
            before = pltpu.roll(jnp.where(row == 7, south, own), 1, axis=0)
            edge_ref[1, at] = jnp.where(own_first, own, 0.5 * (before + own))
        return south

    lax.fori_loop(0, N, gather_b, top, unroll=2)
    remap(1, 3)
    remap(2, 4)
    send_back(BACK_B, REGS_B, ret_b, None)
    scatter(ret_b, back_b, 3)

    mine_a = pltpu.make_async_copy(ret_a.at[me], back_a.at[me], own_sem.at[0])
    mine_b = pltpu.make_async_copy(ret_b.at[me], back_b.at[me], own_sem.at[1])
    mine_a.start()
    mine_b.start()
    everyone(send_a, land_a, 0).wait_send()
    everyone(send_b, land_b, 1).wait_send()
    share.wait_send()
    mine_a.wait()
    mine_b.wait()
    everyone(ret_a, back_a, 2).wait()
    everyone(ret_b, back_b, 3).wait()


def unpack_kernel(eta_ref, back_a, back_b, surface_ref, temp_ref, depth_ref, zonal_ref, merid_ref, phi_ref):
    lane = lanes()
    me = lax.axis_index("lev")
    steps = [eta_ref[2 * me + level + 1] - eta_ref[2 * me + level] for level in range(2)]
    for field, level, offset in BACK_A + BACK_B:
        recv_ref = back_b if field > 2 else back_a
        current = None
        for c in range(N):

            def load(r):
                return recv_ref[c, :, 128 * r : 128 * (r + 1)]

            chunk, start = divmod(BLK * c, 128)
            x = roll_lanes(take(load, offset, BLK, lane), start - offset)
            current = x if start == 0 else jnp.where(lane >= start, x, current)
            if start + BLK < 128:
                continue
            if field == 2:
                for k in range(2):
                    depth_ref[:, k, 128 * chunk : 128 * (chunk + 1)] = steps[k] * current
            else:
                y = current
                if field == 0:
                    y = y + surface_ref[:, 128 * chunk : 128 * (chunk + 1)]
                ref = (phi_ref, temp_ref, None, zonal_ref, merid_ref)[field]
                ref[:, level, 128 * chunk : 128 * (chunk + 1)] = y
            current = x


VMEM = pl.BlockSpec(memory_space=pltpu.VMEM)
SMEM = pl.BlockSpec(memory_space=pltpu.SMEM)


def on_device(temp, depth, zonal, merid, surface, eta, intersection):
    table = intersection[:, :, :, 0, 0]
    block = (LEV, 8, 128)
    backs = pl.pallas_call(
        main_kernel,
        out_shape=[
            jax.ShapeDtypeStruct((N, 8, 128 * REGS_A), F32),
            jax.ShapeDtypeStruct((N, 8, 128 * REGS_B), F32),
        ],
        in_specs=[SMEM, SMEM] + [VMEM] * 4,
        out_specs=[pl.BlockSpec(memory_space=pl.ANY)] * 2,
        scratch_shapes=[
            *[pltpu.VMEM((N, 8, 128 * REGS_F), F32)] * 4,
            pltpu.VMEM((N, 8, 256), F32),
            pltpu.VMEM((N, 8, 128 * REGS_A), F32),
            pltpu.VMEM((N, 8, 128 * REGS_B), F32),
            pltpu.VMEM((3, LEV + 1, 8, 128), F32),
            pltpu.VMEM((3, *block), F32),
            pltpu.VMEM((LEV + 1, 5, 8, 128), F32),
            pltpu.VMEM((5, *block), F32),
            pltpu.SemaphoreType.DMA((5,)),
            pltpu.SemaphoreType.DMA((5,)),
            pltpu.SemaphoreType.DMA((2,)),
        ],
        compiler_params=pltpu.CompilerParams(collective_id=0, has_side_effects=True),
        name="remap",
    )(eta, table, temp, depth, zonal, merid)
    outs = pl.pallas_call(
        unpack_kernel,
        out_shape=[jax.ShapeDtypeStruct((8, 2, LON), F32)] * 5,
        in_specs=[SMEM, VMEM, VMEM, VMEM],
        out_specs=[VMEM] * 5,
        name="unpack",
    )(eta, *backs, surface)
    return tuple(outs)


def solution(mesh):
    shards = P("lat", "lev", None)
    return jax.shard_map(
        on_device,
        mesh=mesh,
        in_specs=(shards,) * 4 + (P("lat", None), P(), P(None, None, None, "lat", "lev")),
        out_specs=(shards,) * 5,
        check_vma=False,
    )
```

time: 101 us -> 64.7 us (0.64)
  blocking collectives: 69.3 us -> 0 us
  Pallas kernels: 28.4 us -> 63.6 us
  waiting for transfers between devices: 1.9 us -> 0 us
    all_to_all x2 -> x0, blocking collectives: 69.3 us -> none  [the longest x1 35.9 us: on_device(): recv = lax.all_to_all(packed, 'lev', 0, 0, tiled=True)]
    pallas_call x2 -> x1, Pallas kernels: 24.5 us -> 59.8 us  [on_device(): pl.pallas_call(main_kernel, out_shape=[jax.ShapeDtypeStruct((N, 8, 128 *...]
    ppermute x1 -> x0, waiting for transfers between devices: 1.9 us -> none  [on_device(): partner = lax.ppermute(recv[:, :, :256], 'lat', [(0, 1), (1, 0)])]
  transfers between devices with their start and end apart: 1 -> 0, of which waited for: 1 -> 0; matrix products, arithmetic and copies ran while one was open for 0% -> 0% of each run, Pallas kernels for 0% -> 0%
where the time goes in v3:
time: 64.7 us; the launch traced here: 64.2 us
  Pallas kernels  63.6 us (98%)
    pallas_call x1, Pallas kernels, on_device(): pl.pallas_call(main_kernel, out_shape=[jax.ShapeDtypeStruct((N, 8, 128 *...  59.8 us
    pallas_call x1, Pallas kernels, on_device(): pl.pallas_call(unpack_kernel, out_shape=[jax.ShapeDtypeStruct((8, 2, LON)...  3.79 us

profile of v3, /device:TPU:0, one launch (start us, length us, event | category | flops | bytes accessed | tf_op | source)
XLA Modules:
  0.0 64.2 jit_solution(8721876706347219659)
XLA Ops:
  0.6 59.8 %remap.1 = (f32[64,8,512]{2,1,0:T(8,128)}, f32[64,8,384]{2,1,0:T(8,128)}) custom-call(f32[129]{0:T(256)} %eta_ref.3, s32[3,2,128]{2,1,0:T(2,128)} %bitcast.1, f32[8,2,5760]{2,1,0:T(2,128)} %temp_ref.1, f32[8,2,5760]{2,1,0:T(2,128)} %depth_ref.1, f32[8,2,5760]{2,1,0:T(2,128)} %zonal_ref.1, f32[8,2,5760]{2,1,0:T(2,128)} %merid_ref.1), custom_call_target="tpu_custom_call" | custom-call | tf_op jit(solution)/shard_map/remap/pallas_call | solution.py:291
  60.4 3.8 %unpack.1 = (f32[8,2,5760]{2,1,0:T(2,128)}, f32[8,2,5760]{2,1,0:T(2,128)}, f32[8,2,5760]{2,1,0:T(2,128)}, f32[8,2,5760]{2,1,0:T(2,128)}, f32[8,2,5760]{2,1,0:T(2,128)}) custom-call(f32[129]{0:T(256)} %eta_ref.3, f32[64,8,512]{2,1,0:T(8,128)} %get-tuple-element.7.back_a, f32[64,8,384]{2,1,0:T(8,128)} %get-tuple-element.8.back_b, f32[8,5760]{1,0:T(8,128)} %surface_ref.1), custom_call_target="tpu_custom_call" | custom-call | tf_op jit(solution)/shard_map/unpack/pallas_call | solution.py:315

commit v4 on v3

v4 whole, which is shorter than its diff:
```python
import functools

import jax
import jax.numpy as jnp
from jax import lax
from jax.experimental import pallas as pl
from jax.experimental.pallas import tpu as pltpu
from jax.sharding import PartitionSpec as P

TOP = 0.2
KAPPA = 0.2857
LEV = 128
LON = 5760
BLK = 90
N = 64
CHUNKS = LON // 128
F32 = jnp.float32

FWD_A = ((1, 0, 0), (1, 1, 91), (0, 0, 182), (0, 1, 272))
FWD_B = ((2, 0, 0), (2, 1, 90), (3, 0, 180), (3, 1, 270))
BACK_A = ((0, 0, 0), (0, 1, 90), (1, 0, 180), (1, 1, 270), (2, 0, 360))
BACK_B = ((3, 0, 0), (3, 1, 90), (4, 0, 180), (4, 1, 270))
REGS_F, REGS_A, REGS_B = 3, 4, 3
MESH = pl.DeviceIdType.MESH


def offsets():
    every = [(x, y, z) for z in range(4) for y in range(4) for x in range(4)][1:]
    order = []
    for d in sorted(every, key=lambda d: -sum(min(v, 4 - v) for v in d)):
        for r in range(3):
            e = d[r:] + d[:r]
            for f in (e, tuple((4 - v) % 4 for v in e)):
                if f not in order:
                    order.append(f)
    return order


OFFSETS = offsets()


def lanes():
    return lax.broadcasted_iota(jnp.int32, (8, 128), 1)


def roll_lanes(x, shift):
    shift = shift % 128
    return x if isinstance(shift, int) and shift == 0 else pltpu.roll(x, shift, axis=1)


def place(regs, piece, offset, width, lane):
    reg, start = divmod(offset, 128)
    regs[reg] = piece if regs[reg] is None else jnp.where(lane >= start, piece, regs[reg])
    if start + width > 128:
        regs[reg + 1] = piece


def take(load, offset, width, lane):
    reg, start = divmod(offset, 128)
    x = load(reg)
    if start + width > 128:
        x = jnp.where(lane >= start, x, load(reg + 1))
    return x


def main_kernel(
    eta_ref, table_ref, temp_hbm, depth_hbm, zonal_hbm, merid_hbm, back_a, back_b,
    temp_ref, depth_ref, zonal_ref, merid_ref,
    send_a, send_b, land_a, land_b, south_ref, ret_a, ret_b,
    edge_ref, par_ref, res_ref, send_sem, recv_sem, own_sem,
):
    lat, me = lax.axis_index("lat"), lax.axis_index("lev")
    lane = lanes()
    row = lax.broadcasted_iota(jnp.int32, (8, 128), 0)
    other = (1 - lat, me)
    loads = [
        pltpu.make_async_copy(src, dst, own_sem.at[i])
        for i, (src, dst) in enumerate(
            ((depth_hbm, depth_ref), (temp_hbm, temp_ref), (zonal_hbm, zonal_ref), (merid_hbm, merid_ref))
        )
    ]
    for c in loads:
        c.start()

    along = [
        [step * lax.rem(at + d, 4) for d in range(4)]
        for step, at in ((1, lax.rem(me, 4)), (4, lax.rem(me // 4, 4)), (16, me // 16))
    ]
    peers = [along[0][x] + along[1][y] + along[2][z] for x, y, z in OFFSETS]
    barrier = pltpu.get_barrier_semaphore()
    for p in peers:
        pl.semaphore_signal(barrier, inc=1, device_id=(lat, p), device_id_type=MESH)
    pl.semaphore_signal(barrier, inc=1, device_id=other, device_id_type=MESH)

    def copy(src, dst, i, device):
        return pltpu.make_async_remote_copy(
            src_ref=src, dst_ref=dst, send_sem=send_sem.at[i], recv_sem=recv_sem.at[i],
            device_id=device, device_id_type=MESH,
        )

    def scatter(src, dst, i):
        for p in peers:
            copy(src.at[p], dst.at[me], i, (lat, p)).start()

    def everyone(src, dst, i):
        return copy(src.at[pl.ds(0, N - 1)], dst.at[pl.ds(0, N - 1)], i, other)

    refs = (temp_ref, depth_ref, zonal_ref, merid_ref)

    def pack(pieces, out):
        def one(c, _):
            regs = [None] * REGS_F
            for field, level, offset in pieces:
                extra = 1 if field == 1 else 0
                first = lax.rem(BLK * c - extra + LON, LON)
                chunk, start = first // 128, lax.rem(first, 128)
                after = lax.rem(chunk + 1, CHUNKS)
                x = refs[field][:, level, pl.ds(pl.multiple_of(128 * chunk, 128), 128)]
                y = refs[field][:, level, pl.ds(pl.multiple_of(128 * after, 128), 128)]
                x = jnp.where(lane >= start, x, y)
                x = pltpu.roll(x, lax.rem(offset % 128 - start + 128, 128), axis=1)
                place(regs, x, offset, BLK + extra, lane)
            for r in range(REGS_F):
                out[c, :, 128 * r : 128 * (r + 1)] = regs[r]
            return 0

        lax.fori_loop(0, N, one, 0, unroll=2)

    loads[0].wait()
    loads[1].wait()
    pack(FWD_A, send_a)
    land_a[me] = send_a[me]
    pl.semaphore_wait(barrier, N)
    scatter(send_a, land_a, 0)
    loads[2].wait()
    loads[3].wait()
    pack(FWD_B, send_b)
    land_b[me] = send_b[me]
    scatter(send_b, land_b, 1)

    top = jnp.full((8, 128), TOP, F32)
    zero = jnp.zeros((8, 128), F32)
    for kind in range(3):
        for p in range(6):
            par_ref[kind, LEV, p] = zero

    def piece(ref, s, offset, width, shift):
        def load(r):
            return ref[s, :, 128 * r : 128 * (r + 1)]

        return roll_lanes(take(load, offset, width, lane), shift - offset)

    def power(x):
        return jnp.exp(KAPPA * jnp.log(x))

    def coefficients(kind, s, above, left, right, q, edge, h):
        bend = q - 0.5 * (left + right)
        par_ref[kind, s, 0] = edge
        par_ref[kind, s, 1] = 1.0 / h
        par_ref[kind, s, 2] = h * left
        par_ref[kind, s, 3] = h * (0.5 * (right - left) + 3.0 * bend)
        par_ref[kind, s, 4] = -2.0 * (h * bend)
        par_ref[kind, s, 5] = above
        return above + h * q

    def layer(kind, s, state, edge_next, q_next, first):
        above, left, q, edge, h, lower = state
        h_next = edge_next - lower
        if first:
            return zero, q_next, q_next, lower, h_next, edge_next
        right = (h_next * q + h * q_next) / (h + h_next)
        above = coefficients(kind, s - 1, above, left, right, q, edge, h)
        return above, right, q_next, lower, h_next, edge_next

    def finish(kind, state):
        above, left, q, edge, h, lower = state
        coefficients(kind, LEV - 1, above, left, q, q, edge, h)
        return lower - TOP

    begin = (zero, zero, zero, zero, zero, top)

    everyone(send_a, land_a, 0).wait_recv()
    share = copy(land_a.at[:, :, pl.ds(0, 256)], south_ref, 4, other)
    share.start()

    def gather_a(s, carry, first=False):
        state, press, work = carry
        for level in range(2):
            x = piece(land_a, s, 91 * level, BLK + 1, -1)
            q = piece(land_a, s, 182 + 90 * level, BLK, 0)
            edge = state[5] + x
            state = layer(0, 2 * s + level, state, edge, q, first and level == 0)
            edge_ref[2 * s + level] = edge
            res_ref[0, 2 * s + level] = work
            below = power(edge)
            work = work + q * (below - press)
            press = below
        return state, press, work

    carry = gather_a(0, (begin, power(top), zero), True)
    state, _, work = lax.fori_loop(1, N, gather_a, carry, unroll=3)
    depth = finish(0, state)

    def remap(kinds, spans):
        def target(k, carry):
            eta0, eta1 = eta_ref[k], eta_ref[k + 1]
            out = []
            for kind, span, before in zip(kinds, spans, carry):
                lower = TOP + eta1 * span
                first = table_ref[kind, 0, k]
                count = table_ref[kind, 1, k]
                mass = par_ref[kind, first, 5]
                for m in range(3):
                    s = first if m == 0 else jnp.where(m < count, first + m, LEV)
                    x = jnp.clip((lower - par_ref[kind, s, 0]) * par_ref[kind, s, 1], 0.0, 1.0)
                    mass = mass + x * (par_ref[kind, s, 2] + x * (par_ref[kind, s, 3] + x * par_ref[kind, s, 4]))
                res_ref[1 + kind, k] = (mass - before) / ((eta1 - eta0) * span)
                out.append(mass)
            return tuple(out)

        lax.fori_loop(0, LEV, target, (zero,) * len(kinds), unroll=4)

    def send_back(pieces, regs_of, out):
        def build(s, _):
            regs = [None] * regs_of
            for field, level, offset in pieces:
                if field == 2:
                    x = depth
                else:
                    x = res_ref[(0, 1, None, 2, 3)[field], 2 * s + level]
                if field == 0:
                    x = work - x
                place(regs, roll_lanes(x, offset), offset, BLK, lane)
            for r in range(regs_of):
                out[s, :, 128 * r : 128 * (r + 1)] = regs[r]
            return 0

        lax.fori_loop(0, N, build, 0, unroll=4)

    mine_a = pltpu.make_async_copy(ret_a.at[me], back_a.at[me], own_sem.at[4])
    mine_b = pltpu.make_async_copy(ret_b.at[me], back_b.at[me], own_sem.at[5])
    remap((0,), (depth,))
    send_back(BACK_A, REGS_A, ret_a)
    scatter(ret_a, back_a, 2)
    mine_a.start()

    share.wait_recv()
    everyone(send_b, land_b, 1).wait_recv()
    own_first = jnp.logical_and(row == 0, lat == 0)

    def gather_b(s, carry, first=False):
        south, zonal, merid = carry
        for level in range(2):
            at = 2 * s + level
            south = south + piece(south_ref, s, 91 * level, BLK + 1, -1)
            own = edge_ref[at]
            before = pltpu.roll(jnp.where(row == 7, south, own), 1, axis=0)
            edge = jnp.where(own_first, own, 0.5 * (before + own))
            zonal = layer(1, at, zonal, edge, piece(land_b, s, 90 * level, BLK, 0), first and level == 0)
            edge = 0.5 * (roll_lanes(own, 1) + own)
            merid = layer(2, at, merid, edge, piece(land_b, s, 180 + 90 * level, BLK, 0), first and level == 0)
        return south, zonal, merid

    carry = gather_b(0, (top, begin, begin), True)
    _, zonal, merid = lax.fori_loop(1, N, gather_b, carry, unroll=3)
    remap((1, 2), (finish(1, zonal), finish(2, merid)))
    send_back(BACK_B, REGS_B, ret_b)
    scatter(ret_b, back_b, 3)
    mine_b.start()

    everyone(send_a, land_a, 0).wait_send()
    everyone(send_b, land_b, 1).wait_send()
    share.wait_send()
    mine_a.wait()
    mine_b.wait()
    everyone(ret_a, back_a, 2).wait()
    everyone(ret_b, back_b, 3).wait()


def unpack_kernel(
    eta_ref, hbm_a, hbm_b, surface_hbm, temp_hbm, depth_hbm, zonal_hbm, merid_hbm, phi_hbm,
    back_a, back_b, surface_ref, out_ref, in_sem, out_sem,
):
    lane = lanes()
    me = lax.axis_index("lev")
    steps = [eta_ref[2 * me + level + 1] - eta_ref[2 * me + level] for level in range(2)]
    loads = [
        pltpu.make_async_copy(src, dst, in_sem.at[i])
        for i, (src, dst) in enumerate(((surface_hbm, surface_ref), (hbm_a, back_a), (hbm_b, back_b)))
    ]
    for c in loads:
        c.start()
    outs = (phi_hbm, temp_hbm, depth_hbm, zonal_hbm, merid_hbm)
    stores = [pltpu.make_async_copy(out_ref.at[i], outs[i], out_sem.at[i]) for i in range(5)]
    loads[0].wait()
    loads[1].wait()
    for i, (field, level, offset) in enumerate(BACK_A + BACK_B):
        if i == len(BACK_A):
            loads[2].wait()
        recv_ref = back_b if field > 2 else back_a
        current = None
        for c in range(N):

            def load(r):
                return recv_ref[c, :, 128 * r : 128 * (r + 1)]

            chunk, start = divmod(BLK * c, 128)
            x = roll_lanes(take(load, offset, BLK, lane), start - offset)
            current = x if start == 0 else jnp.where(lane >= start, x, current)
            if start + BLK < 128:
                continue
            at = slice(128 * chunk, 128 * (chunk + 1))
            if field == 2:
                for k in range(2):
                    out_ref[2, :, k, at] = steps[k] * current
            else:
                y = current + surface_ref[:, at] if field == 0 else current
                out_ref[field, :, level, at] = y
            current = x
        if field == 2 or level == 1:
            stores[field].start()
    for c in stores:
        c.wait()


ANY = pl.BlockSpec(memory_space=pl.ANY)
SMEM = pl.BlockSpec(memory_space=pltpu.SMEM)


def on_device(temp, depth, zonal, merid, surface, eta, intersection):
    table = intersection[:, :, :, 0, 0]
    backs = pl.pallas_call(
        main_kernel,
        out_shape=[
            jax.ShapeDtypeStruct((N, 8, 128 * REGS_A), F32),
            jax.ShapeDtypeStruct((N, 8, 128 * REGS_B), F32),
        ],
        in_specs=[SMEM, SMEM] + [ANY] * 4,
        out_specs=[ANY] * 2,
        scratch_shapes=[
            *[pltpu.VMEM((8, 2, LON), F32)] * 4,
            *[pltpu.VMEM((N, 8, 128 * REGS_F), F32)] * 4,
            pltpu.VMEM((N, 8, 256), F32),
            pltpu.VMEM((N, 8, 128 * REGS_A), F32),
            pltpu.VMEM((N, 8, 128 * REGS_B), F32),
            pltpu.VMEM((LEV, 8, 128), F32),
            pltpu.VMEM((3, LEV + 1, 6, 8, 128), F32),
            pltpu.VMEM((4, LEV, 8, 128), F32),
            pltpu.SemaphoreType.DMA((5,)),
            pltpu.SemaphoreType.DMA((5,)),
            pltpu.SemaphoreType.DMA((6,)),
        ],
        compiler_params=pltpu.CompilerParams(collective_id=0, has_side_effects=True),
        name="remap",
    )(eta, table, temp, depth, zonal, merid)
    outs = pl.pallas_call(
        unpack_kernel,
        out_shape=[jax.ShapeDtypeStruct((8, 2, LON), F32)] * 5,
        in_specs=[SMEM, ANY, ANY, ANY],
        out_specs=[ANY] * 5,
        scratch_shapes=[
            pltpu.VMEM((N, 8, 128 * REGS_A), F32),
            pltpu.VMEM((N, 8, 128 * REGS_B), F32),
            pltpu.VMEM((8, LON), F32),
            pltpu.VMEM((5, 8, 2, LON), F32),
            pltpu.SemaphoreType.DMA((3,)),
            pltpu.SemaphoreType.DMA((5,)),
        ],
        name="unpack",
    )(eta, *backs, surface)
    return tuple(outs)


def solution(mesh):
    shards = P("lat", "lev", None)
    return jax.shard_map(
        on_device,
        mesh=mesh,
        in_specs=(shards,) * 4 + (P("lat", None), P(), P(None, None, None, "lat", "lev")),
        out_specs=(shards,) * 5,
        check_vma=False,
    )
```

time: 64.7 us -> 56.1 us (0.87)
  Pallas kernels: 63.6 us -> 55.2 us
    pallas_call x1, Pallas kernels: 59.8 us -> 51.1 us  [on_device(): pl.pallas_call(main_kernel, out_shape=[jax.ShapeDtypeStruct((N, 8, 128 *...]
where the time goes in v4:
time: 56.1 us; the launch traced here: 55.9 us
  Pallas kernels  55.2 us (98%)
  between operations  0.64 us (1%)
    pallas_call x1, Pallas kernels, on_device(): pl.pallas_call(main_kernel, out_shape=[jax.ShapeDtypeStruct((N, 8, 128 *...  51.1 us
    pallas_call x1, Pallas kernels, on_device(): pl.pallas_call(unpack_kernel, out_shape=[jax.ShapeDtypeStruct((8, 2, LON)...  4.12 us

profile of v4, /device:TPU:0, one launch (start us, length us, event | category | flops | bytes accessed | tf_op | source)
XLA Modules:
  0.0 55.9 jit_solution(17853806146204915460)
XLA Ops:
  0.6 51.1 %remap.1 = (f32[64,8,512]{2,1,0:T(8,128)}, f32[64,8,384]{2,1,0:T(8,128)}) custom-call(f32[129]{0:T(256)} %eta_ref.3, s32[3,2,128]{2,1,0:T(2,128)} %bitcast.1, f32[8,2,5760]{2,1,0:T(2,128)} %temp_hbm.1, f32[8,2,5760]{2,1,0:T(2,128)} %depth_hbm.1, f32[8,2,5760]{2,1,0:T(2,128)} %zonal_hbm.1, f32[8,2,5760]{2,1,0:T(2,128)} %merid_hbm.1), custom_call_target="tpu_custom_call" | custom-call | tf_op jit(solution)/shard_map/remap/pallas_call | solution.py:332
  51.8 4.1 %unpack.1 = (f32[8,2,5760]{2,1,0:T(2,128)}, f32[8,2,5760]{2,1,0:T(2,128)}, f32[8,2,5760]{2,1,0:T(2,128)}, f32[8,2,5760]{2,1,0:T(2,128)}, f32[8,2,5760]{2,1,0:T(2,128)}) custom-call(f32[129]{0:T(256)} %eta_ref.3, f32[64,8,512]{2,1,0:T(8,128)} %get-tuple-element.7.hbm_a, f32[64,8,384]{2,1,0:T(8,128)} %get-tuple-element.8.hbm_b, f32[8,5760]{1,0:T(8,128)} %surface_hbm.1), custom_call_target="tpu_custom_call" | custom-call | tf_op jit(solution)/shard_map/unpack/pallas_call | solution.py:356

commit v5 on v4

--- a/solution.py
+++ b/solution.py
@@ -67,7 +67,7 @@
     eta_ref, table_ref, temp_hbm, depth_hbm, zonal_hbm, merid_hbm, back_a, back_b,
     temp_ref, depth_ref, zonal_ref, merid_ref,
     send_a, send_b, land_a, land_b, south_ref, ret_a, ret_b,
-    edge_ref, par_ref, res_ref, send_sem, recv_sem, own_sem,
+    rows_ref, edge_ref, par_ref, res_ref, send_sem, recv_sem, own_sem,
 ):
     lat, me = lax.axis_index("lat"), lax.axis_index("lev")
     lane = lanes()
@@ -107,33 +107,39 @@
 
     refs = (temp_ref, depth_ref, zonal_ref, merid_ref)
 
+    def spread(fields):
+        def one(chunk, _):
+            for field in fields:
+                for level in range(2):
+                    at = pl.ds(pl.multiple_of(128 * chunk, 128), 128)
+                    rows_ref[2 * field + level, chunk] = refs[field][:, level, at]
+            return 0
+
+        lax.fori_loop(0, CHUNKS, one, 0, unroll=5)
+
     def pack(pieces, out):
-        def one(c, _):
+        for c in range(N):
             regs = [None] * REGS_F
             for field, level, offset in pieces:
                 extra = 1 if field == 1 else 0
-                first = lax.rem(BLK * c - extra + LON, LON)
-                chunk, start = first // 128, lax.rem(first, 128)
-                after = lax.rem(chunk + 1, CHUNKS)
-                x = refs[field][:, level, pl.ds(pl.multiple_of(128 * chunk, 128), 128)]
-                y = refs[field][:, level, pl.ds(pl.multiple_of(128 * after, 128), 128)]
-                x = jnp.where(lane >= start, x, y)
-                x = pltpu.roll(x, lax.rem(offset % 128 - start + 128, 128), axis=1)
-                place(regs, x, offset, BLK + extra, lane)
+                chunk, start = divmod((BLK * c - extra) % LON, 128)
+                x = rows_ref[2 * field + level, chunk]
+                if start + BLK + extra > 128:
+                    x = jnp.where(lane >= start, x, rows_ref[2 * field + level, (chunk + 1) % CHUNKS])
+                place(regs, roll_lanes(x, offset - start), offset, BLK + extra, lane)
             for r in range(REGS_F):
                 out[c, :, 128 * r : 128 * (r + 1)] = regs[r]
-            return 0
-
-        lax.fori_loop(0, N, one, 0, unroll=2)
 
     loads[0].wait()
     loads[1].wait()
+    spread((0, 1))
     pack(FWD_A, send_a)
     land_a[me] = send_a[me]
     pl.semaphore_wait(barrier, N)
     scatter(send_a, land_a, 0)
     loads[2].wait()
     loads[3].wait()
+    spread((2, 3))
     pack(FWD_B, send_b)
     land_b[me] = send_b[me]
     scatter(send_b, land_b, 1)
@@ -237,12 +243,10 @@
 
         lax.fori_loop(0, N, build, 0, unroll=4)
 
-    mine_a = pltpu.make_async_copy(ret_a.at[me], back_a.at[me], own_sem.at[4])
-    mine_b = pltpu.make_async_copy(ret_b.at[me], back_b.at[me], own_sem.at[5])
     remap((0,), (depth,))
     send_back(BACK_A, REGS_A, ret_a)
     scatter(ret_a, back_a, 2)
-    mine_a.start()
+    back_a[me] = ret_a[me]
 
     share.wait_recv()
     everyone(send_b, land_b, 1).wait_recv()
@@ -266,37 +270,30 @@
     remap((1, 2), (finish(1, zonal), finish(2, merid)))
     send_back(BACK_B, REGS_B, ret_b)
     scatter(ret_b, back_b, 3)
-    mine_b.start()
+    back_b[me] = ret_b[me]
 
     everyone(send_a, land_a, 0).wait_send()
     everyone(send_b, land_b, 1).wait_send()
     share.wait_send()
-    mine_a.wait()
-    mine_b.wait()
     everyone(ret_a, back_a, 2).wait()
     everyone(ret_b, back_b, 3).wait()
 
 
 def unpack_kernel(
-    eta_ref, hbm_a, hbm_b, surface_hbm, temp_hbm, depth_hbm, zonal_hbm, merid_hbm, phi_hbm,
-    back_a, back_b, surface_ref, out_ref, in_sem, out_sem,
+    eta_ref, back_a, back_b, surface_hbm, temp_hbm, depth_hbm, zonal_hbm, merid_hbm, phi_hbm,
+    surface_ref, out_ref, in_sem, out_sem,
 ):
     lane = lanes()
     me = lax.axis_index("lev")
     steps = [eta_ref[2 * me + level + 1] - eta_ref[2 * me + level] for level in range(2)]
-    loads = [
-        pltpu.make_async_copy(src, dst, in_sem.at[i])
-        for i, (src, dst) in enumerate(((surface_hbm, surface_ref), (hbm_a, back_a), (hbm_b, back_b)))
-    ]
-    for c in loads:
-        c.start()
+    surface = pltpu.make_async_copy(surface_hbm, surface_ref, in_sem)
+    surface.start()
     outs = (phi_hbm, temp_hbm, depth_hbm, zonal_hbm, merid_hbm)
     stores = [pltpu.make_async_copy(out_ref.at[i], outs[i], out_sem.at[i]) for i in range(5)]
-    loads[0].wait()
-    loads[1].wait()
-    for i, (field, level, offset) in enumerate(BACK_A + BACK_B):
-        if i == len(BACK_A):
-            loads[2].wait()
+    order = BACK_A[2:] + BACK_B + BACK_A[:2]
+    for field, level, offset in order:
+        if (field, level) == (0, 0):
+            surface.wait()
         recv_ref = back_b if field > 2 else back_a
         current = None
         for c in range(N):
@@ -324,6 +321,7 @@
 
 
 ANY = pl.BlockSpec(memory_space=pl.ANY)
+VMEM = pl.BlockSpec(memory_space=pltpu.VMEM)
 SMEM = pl.BlockSpec(memory_space=pltpu.SMEM)
 
 
@@ -332,23 +330,24 @@
     backs = pl.pallas_call(
         main_kernel,
         out_shape=[
-            jax.ShapeDtypeStruct((N, 8, 128 * REGS_A), F32),
-            jax.ShapeDtypeStruct((N, 8, 128 * REGS_B), F32),
+            pltpu.VMEM((N, 8, 128 * REGS_A), F32),
+            pltpu.VMEM((N, 8, 128 * REGS_B), F32),
         ],
         in_specs=[SMEM, SMEM] + [ANY] * 4,
-        out_specs=[ANY] * 2,
+        out_specs=[VMEM] * 2,
         scratch_shapes=[
             *[pltpu.VMEM((8, 2, LON), F32)] * 4,
             *[pltpu.VMEM((N, 8, 128 * REGS_F), F32)] * 4,
             pltpu.VMEM((N, 8, 256), F32),
             pltpu.VMEM((N, 8, 128 * REGS_A), F32),
             pltpu.VMEM((N, 8, 128 * REGS_B), F32),
+            pltpu.VMEM((8, CHUNKS, 8, 128), F32),
             pltpu.VMEM((LEV, 8, 128), F32),
             pltpu.VMEM((3, LEV + 1, 6, 8, 128), F32),
             pltpu.VMEM((4, LEV, 8, 128), F32),
             pltpu.SemaphoreType.DMA((5,)),
             pltpu.SemaphoreType.DMA((5,)),
-            pltpu.SemaphoreType.DMA((6,)),
+            pltpu.SemaphoreType.DMA((4,)),
         ],
         compiler_params=pltpu.CompilerParams(collective_id=0, has_side_effects=True),
         name="remap",
@@ -356,18 +355,16 @@
     outs = pl.pallas_call(
         unpack_kernel,
         out_shape=[jax.ShapeDtypeStruct((8, 2, LON), F32)] * 5,
-        in_specs=[SMEM, ANY, ANY, ANY],
+        in_specs=[SMEM, VMEM, VMEM, ANY],
         out_specs=[ANY] * 5,
         scratch_shapes=[
-            pltpu.VMEM((N, 8, 128 * REGS_A), F32),
-            pltpu.VMEM((N, 8, 128 * REGS_B), F32),
             pltpu.VMEM((8, LON), F32),
             pltpu.VMEM((5, 8, 2, LON), F32),
-            pltpu.SemaphoreType.DMA((3,)),
+            pltpu.SemaphoreType.DMA,
             pltpu.SemaphoreType.DMA((5,)),
         ],
         name="unpack",
-    )(eta, *backs, surface)
+    )(eta, *(pltpu.with_memory_space_constraint(x, pltpu.VMEM) for x in backs), surface)
     return tuple(outs)
 
 

time: 56.1 us -> 53.6 us (0.955)
  Pallas kernels: 55.2 us -> 52.6 us
    pallas_call x1, Pallas kernels: 51.1 us -> 48.9 us  [on_device(): pl.pallas_call(main_kernel, out_shape=[pltpu.VMEM((N, 8, 128 * REGS_A), F...]
where the time goes in v5:
time: 53.6 us; the launch traced here: 53.2 us
  Pallas kernels  52.6 us (98%)
  between operations  0.64 us (1%)
    pallas_call x1, Pallas kernels, on_device(): pl.pallas_call(main_kernel, out_shape=[pltpu.VMEM((N, 8, 128 * REGS_A), F...  48.9 us
    pallas_call x1, Pallas kernels, on_device(): pl.pallas_call(unpack_kernel, out_shape=[jax.ShapeDtypeStruct((8, 2, LON)...  3.63 us

profile of v5, /device:TPU:0, one launch (start us, length us, event | category | flops | bytes accessed | tf_op | source)
XLA Modules:
  0.0 53.2 jit_solution(17555803542649493671)
XLA Ops:
  0.6 48.9 %remap.1 = (f32[64,8,512]{2,1,0:T(8,128)S(1)}, f32[64,8,384]{2,1,0:T(8,128)S(1)}) custom-call(f32[129]{0:T(256)} %eta_ref.3, s32[3,2,128]{2,1,0:T(2,128)} %bitcast.1, f32[8,2,5760]{2,1,0:T(2,128)} %temp_hbm.1, f32[8,2,5760]{2,1,0:T(2,128)} %depth_hbm.1, f32[8,2,5760]{2,1,0:T(2,128)} %zonal_hbm.1, f32[8,2,5760]{2,1,0:T(2,128)} %merid_hbm.1), custom_call_target="tpu_custom_call" | custom-call | tf_op jit(solution)/shard_map/remap/pallas_call | solution.py:330
  49.6 3.6 %unpack.1 = (f32[8,2,5760]{2,1,0:T(2,128)}, f32[8,2,5760]{2,1,0:T(2,128)}, f32[8,2,5760]{2,1,0:T(2,128)}, f32[8,2,5760]{2,1,0:T(2,128)}, f32[8,2,5760]{2,1,0:T(2,128)}) custom-call(f32[129]{0:T(256)} %eta_ref.3, f32[64,8,512]{2,1,0:T(8,128)S(1)} %get-tuple-element.7.back_a, f32[64,8,384]{2,1,0:T(8,128)S(1)} %get-tuple-element.8.back_b, f32[8,5760]{1,0:T(8,128)} %surface_hbm.1), custom_call_target="tpu_custom_call" | custom-call | tf_op jit(solution)/shard_map/unpack/pallas_call | solution.py:355

commit v6 on v5

--- a/solution.py
+++ b/solution.py
@@ -18,9 +18,10 @@
 
 FWD_A = ((1, 0, 0), (1, 1, 91), (0, 0, 182), (0, 1, 272))
 FWD_B = ((2, 0, 0), (2, 1, 90), (3, 0, 180), (3, 1, 270))
-BACK_A = ((0, 0, 0), (0, 1, 90), (1, 0, 180), (1, 1, 270), (2, 0, 360))
+BACK_A = ((0, 0, 0), (0, 1, 90), (1, 0, 180), (1, 1, 270))
 BACK_B = ((3, 0, 0), (3, 1, 90), (4, 0, 180), (4, 1, 270))
-REGS_F, REGS_A, REGS_B = 3, 4, 3
+REGS_F = REGS_A = REGS_B = 3
+FREE = 24
 MESH = pl.DeviceIdType.MESH
 
 
@@ -64,9 +65,9 @@
 
 
 def main_kernel(
-    eta_ref, table_ref, temp_hbm, depth_hbm, zonal_hbm, merid_hbm, back_a, back_b,
+    eta_ref, table_ref, temp_hbm, depth_hbm, zonal_hbm, merid_hbm, back_a, back_b, back_t,
     temp_ref, depth_ref, zonal_ref, merid_ref,
-    send_a, send_b, land_a, land_b, south_ref, ret_a, ret_b,
+    send_a, send_b, land_a, land_b, south_ref, ret_a, ret_b, ret_t,
     rows_ref, edge_ref, par_ref, res_ref, send_sem, recv_sem, own_sem,
 ):
     lat, me = lax.axis_index("lat"), lax.axis_index("lev")
@@ -206,6 +207,9 @@
     carry = gather_a(0, (begin, power(top), zero), True)
     state, _, work = lax.fori_loop(1, N, gather_a, carry, unroll=3)
     depth = finish(0, state)
+    rest = roll_lanes(depth, -2 * FREE)
+    rest = jnp.where(lane < 64, rest, roll_lanes(pltpu.roll(rest, 4, axis=0), 64))
+    ret_t[...] = rest[0:4]
 
     def remap(kinds, spans):
         def target(k, carry):
@@ -226,25 +230,26 @@
 
         lax.fori_loop(0, LEV, target, (zero,) * len(kinds), unroll=4)
 
-    def send_back(pieces, regs_of, out):
+    def send_back(pieces, regs_of, out, extra):
         def build(s, _):
             regs = [None] * regs_of
             for field, level, offset in pieces:
-                if field == 2:
-                    x = depth
-                else:
-                    x = res_ref[(0, 1, None, 2, 3)[field], 2 * s + level]
+                x = res_ref[(0, 1, None, 2, 3)[field], 2 * s + level]
                 if field == 0:
                     x = work - x
                 place(regs, roll_lanes(x, offset), offset, BLK, lane)
+            regs[-1] = jnp.where(lane >= 128 - FREE, extra, regs[-1])
             for r in range(regs_of):
                 out[s, :, 128 * r : 128 * (r + 1)] = regs[r]
             return 0
 
         lax.fori_loop(0, N, build, 0, unroll=4)
 
+    back_t[me] = ret_t[...]
+    for p in peers:
+        copy(ret_t, back_t.at[me], 5, (lat, p)).start()
     remap((0,), (depth,))
-    send_back(BACK_A, REGS_A, ret_a)
+    send_back(BACK_A, REGS_A, ret_a, roll_lanes(depth, -FREE))
     scatter(ret_a, back_a, 2)
     back_a[me] = ret_a[me]
 
@@ -268,7 +273,7 @@
     carry = gather_b(0, (top, begin, begin), True)
     _, zonal, merid = lax.fori_loop(1, N, gather_b, carry, unroll=3)
     remap((1, 2), (finish(1, zonal), finish(2, merid)))
-    send_back(BACK_B, REGS_B, ret_b)
+    send_back(BACK_B, REGS_B, ret_b, roll_lanes(depth, -2 * FREE))
     scatter(ret_b, back_b, 3)
     back_b[me] = ret_b[me]
 
@@ -277,11 +282,13 @@
     share.wait_send()
     everyone(ret_a, back_a, 2).wait()
     everyone(ret_b, back_b, 3).wait()
+    rests = copy(back_t.at[pl.ds(0, N - 1)], back_t.at[pl.ds(0, N - 1)], 5, other)
+    rests.wait()
 
 
 def unpack_kernel(
-    eta_ref, back_a, back_b, surface_hbm, temp_hbm, depth_hbm, zonal_hbm, merid_hbm, phi_hbm,
-    surface_ref, out_ref, in_sem, out_sem,
+    eta_ref, back_a, back_b, back_t, surface_hbm, temp_hbm, depth_hbm, zonal_hbm, merid_hbm, phi_hbm,
+    surface_ref, span_ref, out_ref, in_sem, out_sem,
 ):
     lane = lanes()
     me = lax.axis_index("lev")
@@ -290,7 +297,21 @@
     surface.start()
     outs = (phi_hbm, temp_hbm, depth_hbm, zonal_hbm, merid_hbm)
     stores = [pltpu.make_async_copy(out_ref.at[i], outs[i], out_sem.at[i]) for i in range(5)]
-    order = BACK_A[2:] + BACK_B + BACK_A[:2]
+    row = lax.broadcasted_iota(jnp.int32, (8, 128), 0)
+
+    def spans(g, _):
+        pair = back_t[g]
+        swapped = pltpu.roll(pair, 4, axis=0)
+        for k, (upper, lower) in enumerate(((pair, swapped), (swapped, pair))):
+            first = roll_lanes(back_a[2 * g + k, :, 256:384], FREE)
+            second = roll_lanes(back_b[2 * g + k, :, 256:384], 2 * FREE)
+            rest = jnp.where(row < 4, roll_lanes(upper, 2 * FREE), roll_lanes(lower, 2 * FREE + 64))
+            x = jnp.where(lane < FREE, first, jnp.where(lane < 2 * FREE, second, rest))
+            span_ref[2 * g + k] = x
+        return 0
+
+    lax.fori_loop(0, N // 2, spans, 0, unroll=16)
+    order = BACK_A[2:] + BACK_B + ((2, 0, 0),) + BACK_A[:2]
     for field, level, offset in order:
         if (field, level) == (0, 0):
             surface.wait()
@@ -302,7 +323,8 @@
                 return recv_ref[c, :, 128 * r : 128 * (r + 1)]
 
             chunk, start = divmod(BLK * c, 128)
-            x = roll_lanes(take(load, offset, BLK, lane), start - offset)
+            x = span_ref[c] if field == 2 else take(load, offset, BLK, lane)
+            x = roll_lanes(x, start - offset)
             current = x if start == 0 else jnp.where(lane >= start, x, current)
             if start + BLK < 128:
                 continue
@@ -332,33 +354,37 @@
         out_shape=[
             pltpu.VMEM((N, 8, 128 * REGS_A), F32),
             pltpu.VMEM((N, 8, 128 * REGS_B), F32),
+            pltpu.VMEM((N, 4, 128), F32),
         ],
         in_specs=[SMEM, SMEM] + [ANY] * 4,
-        out_specs=[VMEM] * 2,
+        out_specs=[VMEM] * 3,
         scratch_shapes=[
             *[pltpu.VMEM((8, 2, LON), F32)] * 4,
             *[pltpu.VMEM((N, 8, 128 * REGS_F), F32)] * 4,
             pltpu.VMEM((N, 8, 256), F32),
             pltpu.VMEM((N, 8, 128 * REGS_A), F32),
             pltpu.VMEM((N, 8, 128 * REGS_B), F32),
+            pltpu.VMEM((4, 128), F32),
             pltpu.VMEM((8, CHUNKS, 8, 128), F32),
             pltpu.VMEM((LEV, 8, 128), F32),
             pltpu.VMEM((3, LEV + 1, 6, 8, 128), F32),
             pltpu.VMEM((4, LEV, 8, 128), F32),
-            pltpu.SemaphoreType.DMA((5,)),
-            pltpu.SemaphoreType.DMA((5,)),
+            pltpu.SemaphoreType.DMA((6,)),
+            pltpu.SemaphoreType.DMA((6,)),
             pltpu.SemaphoreType.DMA((4,)),
         ],
         compiler_params=pltpu.CompilerParams(collective_id=0, has_side_effects=True),
         name="remap",
     )(eta, table, temp, depth, zonal, merid)
+    backs = [backs[0], backs[1], backs[2].reshape(N // 2, 8, 128)]
     outs = pl.pallas_call(
         unpack_kernel,
         out_shape=[jax.ShapeDtypeStruct((8, 2, LON), F32)] * 5,
-        in_specs=[SMEM, VMEM, VMEM, ANY],
+        in_specs=[SMEM, VMEM, VMEM, VMEM, ANY],
         out_specs=[ANY] * 5,
         scratch_shapes=[
             pltpu.VMEM((8, LON), F32),
+            pltpu.VMEM((N, 8, 128), F32),
             pltpu.VMEM((5, 8, 2, LON), F32),
             pltpu.SemaphoreType.DMA,
             pltpu.SemaphoreType.DMA((5,)),

time: 53.6 us -> 52.3 us (0.976)
  Pallas kernels: 52.6 us -> 50.7 us
    pallas_call x1, Pallas kernels: 48.9 us -> 47.6 us  [on_device(): pl.pallas_call(main_kernel, out_shape=[pltpu.VMEM((N, 8, 128 * REGS_A), F...]
where the time goes in v6:
time: 52.3 us; the launch traced here: 51.4 us
  Pallas kernels  50.7 us (97%)
  between operations  0.64 us (1%)
    pallas_call x1, Pallas kernels, on_device(): pl.pallas_call(main_kernel, out_shape=[pltpu.VMEM((N, 8, 128 * REGS_A), F...  47.6 us
    pallas_call x1, Pallas kernels, on_device(): pl.pallas_call(unpack_kernel, out_shape=[jax.ShapeDtypeStruct((8, 2, LON)...  3.17 us

profile of v6, /device:TPU:0, one launch (start us, length us, event | category | flops | bytes accessed | tf_op | source)
XLA Modules:
  0.0 51.4 jit_solution(8470121044209309992)
XLA Ops:
  0.6 47.6 %remap.1 = (f32[64,8,384]{2,1,0:T(8,128)S(1)}, f32[64,8,384]{2,1,0:T(8,128)S(1)}, f32[64,4,128]{2,1,0:T(4,128)S(1)}) custom-call(f32[129]{0:T(256)} %eta_ref.3, s32[3,2,128]{2,1,0:T(2,128)} %bitcast.3, f32[8,2,5760]{2,1,0:T(2,128)} %temp_hbm.1, f32[8,2,5760]{2,1,0:T(2,128)} %depth_hbm.1, f32[8,2,5760]{2,1,0:T(2,128)} %zonal_hbm.1, f32[8,2,5760]{2,1,0:T(2,128)} %merid_hbm.1), custom_call_target="tpu_custom_call" | custom-call | tf_op jit(solution)/shard_map/remap/pallas_call | solution.py:352
  48.2 3.2 %unpack.1 = (f32[8,2,5760]{2,1,0:T(2,128)}, f32[8,2,5760]{2,1,0:T(2,128)}, f32[8,2,5760]{2,1,0:T(2,128)}, f32[8,2,5760]{2,1,0:T(2,128)}, f32[8,2,5760]{2,1,0:T(2,128)}) custom-call(f32[129]{0:T(256)} %eta_ref.3, f32[64,8,384]{2,1,0:T(8,128)S(1)} %get-tuple-element.8.back_a, f32[64,8,384]{2,1,0:T(8,128)S(1)} %get-tuple-element.9.back_b, ...), custom_call_target="tpu_custom_call" | custom-call | tf_op jit(solution)/shard_map/unpack/pallas_call | solution.py:380

commit v7 on v6

--- a/solution.py
+++ b/solution.py
@@ -80,11 +80,11 @@
             ((depth_hbm, depth_ref), (temp_hbm, temp_ref), (zonal_hbm, zonal_ref), (merid_hbm, merid_ref))
         )
     ]
-    for c in loads:
+    for c in loads[:2]:
         c.start()
 
     along = [
-        [step * lax.rem(at + d, 4) for d in range(4)]
+        [step * lax.rem(at + d + 2 * d * lat, 4) for d in range(4)]
         for step, at in ((1, lax.rem(me, 4)), (4, lax.rem(me // 4, 4)), (16, me // 16))
     ]
     peers = [along[0][x] + along[1][y] + along[2][z] for x, y, z in OFFSETS]
@@ -92,6 +92,8 @@
     for p in peers:
         pl.semaphore_signal(barrier, inc=1, device_id=(lat, p), device_id_type=MESH)
     pl.semaphore_signal(barrier, inc=1, device_id=other, device_id_type=MESH)
+    for c in loads[2:]:
+        c.start()
 
     def copy(src, dst, i, device):
         return pltpu.make_async_remote_copy(
@@ -116,7 +118,7 @@
                     rows_ref[2 * field + level, chunk] = refs[field][:, level, at]
             return 0
 
-        lax.fori_loop(0, CHUNKS, one, 0, unroll=5)
+        lax.fori_loop(0, CHUNKS, one, 0, unroll=9)
 
     def pack(pieces, out):
         for c in range(N):
@@ -132,8 +134,9 @@
                 out[c, :, 128 * r : 128 * (r + 1)] = regs[r]
 
     loads[0].wait()
+    spread((1,))
     loads[1].wait()
-    spread((0, 1))
+    spread((0,))
     pack(FWD_A, send_a)
     land_a[me] = send_a[me]
     pl.semaphore_wait(barrier, N)

time: 52.3 us -> 52.3 us (level)
  no operation moved by 1% of the time
where the time goes in v7:
time: 52.3 us; the launch traced here: 51.7 us
  Pallas kernels  51.1 us (98%)
  between operations  0.64 us (1%)
    pallas_call x1, Pallas kernels, on_device(): pl.pallas_call(main_kernel, out_shape=[pltpu.VMEM((N, 8, 128 * REGS_A), F...  47.9 us
    pallas_call x1, Pallas kernels, on_device(): pl.pallas_call(unpack_kernel, out_shape=[jax.ShapeDtypeStruct((8, 2, LON)...  3.17 us

profile of v7, /device:TPU:0, one launch (start us, length us, event | category | flops | bytes accessed | tf_op | source)
XLA Modules:
  0.0 51.7 jit_solution(8045791757578426961)
XLA Ops:
  0.6 47.9 %remap.1 = (f32[64,8,384]{2,1,0:T(8,128)S(1)}, f32[64,8,384]{2,1,0:T(8,128)S(1)}, f32[64,4,128]{2,1,0:T(4,128)S(1)}) custom-call(f32[129]{0:T(256)} %eta_ref.3, s32[3,2,128]{2,1,0:T(2,128)} %bitcast.3, f32[8,2,5760]{2,1,0:T(2,128)} %temp_hbm.1, f32[8,2,5760]{2,1,0:T(2,128)} %depth_hbm.1, f32[8,2,5760]{2,1,0:T(2,128)} %zonal_hbm.1, f32[8,2,5760]{2,1,0:T(2,128)} %merid_hbm.1), custom_call_target="tpu_custom_call" | custom-call | tf_op jit(solution)/shard_map/remap/pallas_call | solution.py:355
  48.6 3.2 %unpack.1 = (f32[8,2,5760]{2,1,0:T(2,128)}, f32[8,2,5760]{2,1,0:T(2,128)}, f32[8,2,5760]{2,1,0:T(2,128)}, f32[8,2,5760]{2,1,0:T(2,128)}, f32[8,2,5760]{2,1,0:T(2,128)}) custom-call(f32[129]{0:T(256)} %eta_ref.3, f32[64,8,384]{2,1,0:T(8,128)S(1)} %get-tuple-element.8.back_a, f32[64,8,384]{2,1,0:T(8,128)S(1)} %get-tuple-element.9.back_b, ...), custom_call_target="tpu_custom_call" | custom-call | tf_op jit(solution)/shard_map/unpack/pallas_call | solution.py:383
